TPU v7x, 256 devices: a whole 4x4x8 slice. The times are simulated.
256 devices in a mesh: band: 32 (over y_hi, z, core), fft: 8 (over x, y_lo).
Axes of the slice: x: 4, y: 4 (y_hi: 2, y_lo: 2; y = y_hi * 2 + y_lo), z: 8, core: 2. Of those that a mesh axis runs over, the one named last changes fastest.
Arguments:
- coefficients: float32 [32, 2, 72, 5184], P('band', None, None, 'fft'), may hold values from -0.009765625 to 0.009765625
- col_index: int32 [5184], replicated, may hold values from 0 to 5183, each once
- occupation: int32 [32], P('band'), may hold values from 1 to 4
Outputs:
- density: float32 [288, 288, 288], P('band', 'fft')
Inputs may be any that keep to these rules, and one draw needn't show every extreme that they name: `col_index`: each number of the range appears once.
All inputs are finite; a program needn't handle non-finite values.
Results may differ from a plain program's by a relative error of at most 0.0003.
Values sent between devices are 32-bit elements; how exact they have to be, the bound alone decides.
No kernel may reach another device: no remote copies, remote signals or barrier semaphores. Data moves between devices by JAX's collectives and lax.ppermute only.
A program may use at most 64 MiB of HBM per device.

v0:
```python
import math

import jax
import jax.numpy as jnp
from jax import lax
from jax.sharding import PartitionSpec as P

NC = 144
NF = 288
KZ = 72
NCOLS = 5184


def split_up(value, dim, count):
    before, after = (value.shape[:dim], value.shape[dim + 1 :])
    return jnp.moveaxis(value.reshape(*before, count, -1, *after), dim, 0)


def sum_at_owner(value, axis, dim):
    parts = split_up(value, dim, lax.axis_size(axis))
    arrived = lax.all_to_all(parts, axis, split_axis=0, concat_axis=0, tiled=True)
    return arrived.sum(axis=0)


def product(pattern, operand_a, operand_b):
    return jnp.einsum(pattern, operand_a, operand_b, precision=lax.Precision.HIGHEST)


def phase_tables(wave_count, offset, points):
    wave_index = jnp.arange(wave_count, dtype=jnp.int32) - offset
    grid_index = jnp.arange(points, dtype=jnp.int32)
    phases = jnp.mod(wave_index[:, None] * grid_index[None, :], points)
    angles = phases.astype(jnp.float32) * (2.0 * math.pi / points)
    return (jnp.cos(angles), jnp.sin(angles))


def interpolation_matrix(coarse_len, fine_len):
    fine_index = jnp.arange(fine_len, dtype=jnp.int32)
    coarse_index = jnp.arange(coarse_len, dtype=jnp.int32)
    wave_index = jnp.arange(1, coarse_len // 2, dtype=jnp.int32)
    offsets = fine_index[:, None] - 2 * coarse_index[None, :]
    phases = jnp.mod(offsets[:, :, None] * wave_index[None, None, :], fine_len)
    angles = phases.astype(jnp.float32) * (2.0 * math.pi / fine_len)
    return (1.0 + 2.0 * jnp.sum(jnp.cos(angles), axis=2)) / coarse_len


def rotate(pattern, real_part, imag_part, cos_table, sin_table):
    out_real = product(pattern, real_part, cos_table) - product(pattern, imag_part, sin_table)
    out_imag = product(pattern, real_part, sin_table) + product(pattern, imag_part, cos_table)
    return (out_real, out_imag)


def local(coefficients, col_index, occupation):
    band_here = coefficients.shape[0]
    col_count = coefficients.shape[3]
    band_total = band_here * lax.axis_size("band")
    radius = KZ // 2
    col_start = lax.axis_index("fft") * col_count
    local_cols = lax.dynamic_slice_in_dim(col_index, col_start, col_count)
    first_wave = local_cols // KZ - radius
    second_wave = local_cols % KZ - radius
    third_wave = jnp.arange(KZ, dtype=jnp.int32) - radius
    radial = (first_wave * first_wave + second_wave * second_wave)[None, :] + (
        third_wave * third_wave
    )[:, None]
    inside = (radial <= radius * radius).astype(jnp.float32)
    masked = coefficients * inside
    cos_table, sin_table = phase_tables(KZ, radius, NC)
    line_real, line_imag = rotate("bkc,kz->bzc", masked[:, 0], masked[:, 1], cos_table, sin_table)
    z_lines = jnp.stack([line_real, line_imag], axis=1)
    inverse = jnp.zeros((NCOLS,), jnp.int32).at[col_index].set(jnp.arange(NCOLS, dtype=jnp.int32))
    block_in = lax.all_to_all(z_lines, "fft", split_axis=2, concat_axis=3, tiled=True)
    box_grid = jnp.take(block_in, inverse, axis=3)
    box_grid = box_grid.reshape(block_in.shape[0], 2, block_in.shape[2], KZ, KZ)
    half_real, half_imag = rotate(
        "bzak,kr->bzar", box_grid[:, 0], box_grid[:, 1], cos_table, sin_table
    )
    full_real, full_imag = rotate("bzar,as->bzsr", half_real, half_imag, cos_table, sin_table)
    moduli = full_real * full_real + full_imag * full_imag
    weights = occupation.astype(jnp.float32) / band_total
    partial_value = product("b,bzxy->zxy", weights, moduli)
    interpolation = interpolation_matrix(NC, NF)
    section_one = product("zab,ga->zgb", partial_value, interpolation)
    shared = sum_at_owner(section_one, "band", 1)
    reduced = product("zgb,fb->zgf", shared, interpolation)
    return product(
        "rgf,hr->gfh",
        lax.all_to_all(reduced, "fft", split_axis=2, concat_axis=0, tiled=True),
        interpolation,
    )


def solution(mesh):
    return jax.shard_map(
        local,
        mesh=mesh,
        in_specs=(P("band", None, None, "fft"), P(), P("band")),
        out_specs=P("band", "fft", None),
        check_vma=False,
    )
```

profile of v0, /device:TPU:32, one launch (start us, length us, event | category | flops | bytes accessed | tf_op | source)
XLA Modules:
  0.0 300.1 jit_solution(10613181250059869739)
XLA Ops:
  0.9 1.1 broadcast_multiply_fusion
  3.6 0.8 fusion.8
  4.4 0.8 fusion.7
  5.3 1.6 copy.37
  6.9 5.3 %all-to-all-start = ((f32[1,2,144,648]{3,1,0,2:T(2,128)}), f32[1,2,144,648]{3,1,0,2:T(2,128)S(1)}, u32[]{:S(2)}, u32[]{:S(2)}) async-start(f32[1,2,144,648]{3,1,0,2:T(2,128)} %copy.37), calls=%async_computation | async-start | bytes 1769472 | tf_op jit(solution)/shard_map/all_to_all | solution.py:72
  12.2 25.5 %scatter_custom_fusion = s32[5184]{0:T(1024)S(1)} fusion(s32[5184]{0:T(1024)S(1)} %compare_select_fusion.1, s32[5184]{0:T(1024)S(1)} %iota.59, s32[]{:T(128)} %constant.51.clone.1), kind=kCustom, calls=%fused_computation.107 | custom fusion | bytes 20740 | tf_op jit(solution)/shard_map/scatter | solution.py:71
  38.6 61.0 %fusion.3 = f32[288,144]{0,1:T(8,128)S(1)} fusion(s32[71]{0:T(128)S(1)} %iota_add_fusion.1, s32[288,144]{0,1:T(8,128)S(1)} %iota_subtract_fusion), kind=kLoop, calls=%fused_computation.6 | loop fusion | flops 29403648 | bytes 332060 | tf_op jit(solution)/shard_map/reduce_sum | solution.py:44
  99.6 4.8 %copy.56 = f32[1,2,18,8,648]{2,1,4,3,0:T(2,128)} copy(f32[1,2,18,8,648]{4,1,2,3,0:T(2,128)S(1)} %bitcast.93) | data formatting | bytes 1492992 | tf_op jit(solution)/shard_map/all_to_all | solution.py:72
  104.4 19.3 %gather_fusion = f32[5184,2,18]{2,1,0:T(2,128)} fusion(f32[2,18,5184]{1,0,2:T(2,128)} %bitcast.92, s32[6144]{0:T(1024)S(1)} %pad_clamp_fusion), kind=kCustom, calls=%fused_computation | custom fusion | bytes 1513728 | tf_op jit(solution)/shard_map/jit(_take)/gather | solution.py:73
  123.7 7.0 %copy.41 = f32[1,2,18,72,72]{4,3,2,1,0:T(8,128)S(1)} copy(f32[1,2,18,72,72]{2,1,4,3,0:T(2,128)} %bitcast.91) | data formatting | bytes 1492992 | tf_op jit(solution)/shard_map/jit(_take)/gather | solution.py:73
  130.8 1.5 fusion.9
  132.3 1.5 fusion.10
  133.8 1.5 convolution_subtract_fusion
  135.3 2.5 fusion.39
  137.8 2.5 fusion.31
  140.3 1.5 convolution_add_fusion
  141.9 2.7 fusion.33
  144.6 3.2 %multiply_bitcast_fusion = f32[18,144,144]{2,1,0:T(8,128)S(1)} fusion(f32[144,18,144]{2,0,1:T(8,128)S(1)} %fusion.31, f32[144,18,144]{2,0,1:T(8,128)S(1)} %fusion.39, f32[144,18,144]{2,0,1:T(8,128)S(1)} %fusion.33, f32[18,72,144]{2,1,0:T(8,128)S(1)} %convolution_add_fusion, f32[]{:T(128)} %bitcast, s32[72]{0:T(128)S(1)} %iota_add_fusion), kind=kOutput, calls=%fused_computation.11 | convolution fusion | flops 324819072 | bytes 6718756 | tf_op jit(solution)/shard_map/bzar,as->bzsr/dot_general | solution.py:26
  147.8 2.6 copy.46
  150.4 8.1 %fusion.18 = f32[288,2592]{0,1} fusion(f32[144,2592]{0,1:T(8,128)} %bitcast.88, f32[288,144]{0,1:T(8,128)S(1)} %fusion.3), kind=kOutput, calls=%fused_computation.37 | convolution fusion | flops 1290069504 | bytes 4644864
  158.4 8.5 %copy.47 = f32[18,288,144]{2,0,1:T(8,128)} copy(f32[18,288,144]{1,2,0:T(8,128)} %bitcast.87) | data formatting | bytes 5971968 | tf_op jit(solution)/shard_map/zab,ga->zgb/transpose | solution.py:26
  166.9 8.6 %reshape.196 = f32[32,1,23328]{2,1,0:T(1,128)} reshape(f32[32,9,18,144]{3,2,1,0:T(8,128)} %bitcast.86) | data formatting | bytes 5971968
  175.5 83.3 %all_to_all.41 = f32[32,1,23328]{2,1,0:T(1,128)S(1)} all-to-all(f32[32,1,23328]{2,1,0:T(1,128)} %reshape.196), channel_id=1, replica_groups=mesh['band'=32,'fft'=8] {'band'}, dimensions={0} | all-to-all | bytes 5971968 | tf_op jit(solution)/shard_map/all_to_all | solution.py:21
  259.3 10.2 %reduce = f32[32,23328]{1,0:T(8,128)} reduce(f32[32,1,23328]{2,1,0:T(1,128)S(1)} %all_to_all.41, f32[]{:T(128)} %broadcast.120), dimensions={1}, to_apply=%all_to_all.33.reduce_sub_computation | reduce | bytes 5971972 | tf_op jit(solution)/shard_map/all_to_all | solution.py:21
  269.5 7.1 %reshape.197 = f32[32,9,18,144]{3,2,1,0:T(8,128)} reshape(f32[32,23328]{1,0:T(8,128)} %reduce) | data formatting | bytes 5971968
  276.6 3.5 %bitcast_reduce_fusion = f32[18,9,144]{2,0,1:T(8,128)S(1)} fusion(f32[32,9,18,144]{3,2,1,0:T(8,128)} %reshape.197), kind=kLoop, calls=%fused_computation.168 | loop fusion | flops 723168 | bytes 3079296 | tf_op jit(solution)/shard_map/reduce_sum | solution.py:22
  280.7 1.4 copy.48
  282.1 0.9 reshape.198
  283.0 11.5 %all_to_all.42 = f32[8,1,5832]{2,1,0:T(1,128)S(1)} all-to-all(f32[8,1,5832]{2,1,0:T(1,128)S(1)} %reshape.198), channel_id=1, replica_groups=mesh['band'=32,'fft'=8] {'fft'}, dimensions={0} | all-to-all | bytes 373248 | tf_op jit(solution)/shard_map/all_to_all | solution.py:88
  294.5 1.1 reduce.1
  296.4 1.0 copy.49
  297.4 2.4 fusion.11
  (24 shorter events, 4.7 us)
Async XLA Ops:
  5.2 7.0 %copy-start = (s32[5184]{0:T(1024)S(1)}, s32[5184]{0:T(1024)}, u32[]{:S(2)}) copy-start(s32[5184]{0:T(1024)} %param.4) | copy-start | bytes 62212
  6.9 92.7 %all-to-all-start = ((f32[1,2,144,648]{3,1,0,2:T(2,128)}), f32[1,2,144,648]{3,1,0,2:T(2,128)S(1)}, u32[]{:S(2)}, u32[]{:S(2)}) async-start(f32[1,2,144,648]{3,1,0,2:T(2,128)} %copy.37), calls=%async_computation | async-start | bytes 1769472 | tf_op jit(solution)/shard_map/all_to_all | solution.py:72
where the time goes:
time: 305 us; the launch traced here: 300 us
  blocking collectives  94.8 us (31%)
  local copies, waits for them, and re-layouts  89.6 us (29%)
  other arithmetic  78.1 us (26%)
  matrix products  31.1 us (10%)
  starting transfers between devices  5.3 us (2%)
    all_to_all x1, blocking collectives, sum_at_owner(): lax.all_to_all(parts, axis, split_axis=0, concat_axis=0, tiled=True)  83.3 us
    reduce_sum x1, other arithmetic, interpolation_matrix(): return (1.0 + 2.0 * jnp.sum(jnp.cos(angles), axis=2)) / coarse_len  61 us
    gather x2, local copies, waits for them, and re-layouts, local(): box_grid = jnp.take(block_in, inverse, axis=3)  26.2 us
    scatter x1, local copies, waits for them, and re-layouts, local(): jnp.zeros((NCOLS,), jnp.int32).at[col_index]  25.5 us
    dot_general x14, matrix products, product(): jnp.einsum(pattern, operand_a, operand_b, precision=lax.Precision.HIGHEST)  23 us
    unnamed x6, local copies, waits for them, and re-layouts  17.3 us
    all_to_all x1, blocking collectives, local(): lax.all_to_all(reduced, 'fft', split_axis=2, concat_axis=0, tiled=True)  11.5 us
    all_to_all x1, other arithmetic, sum_at_owner(): lax.all_to_all(parts, axis, split_axis=0, concat_axis=0, tiled=True)  10.2 us
  transfers between devices with their start and end apart: 1, of which 0 were waited for; matrix products, arithmetic and copies ran while one was open for 29% of the time, Pallas kernels for 0%

commit v1 on v0

v1 whole, which is shorter than its diff:
```python
import jax
import jax.numpy as jnp
import ml_dtypes
import numpy as np
from jax import lax
from jax.experimental import pallas as pl
from jax.experimental.pallas import tpu as pltpu
from jax.sharding import Mesh, PartitionSpec as P

NC = 144
NF = 288
KZ = 72
NCOLS = 5184
BANDS = 32
R2 = (KZ // 2) ** 2

AXES = ("yh", "z", "core", "x", "yl")
SIZES = (2, 8, 2, 4, 2)
PLANE = ("yh", "x", "yl")
NP = NC // 16
CB = NCOLS // 8
GR = 96
NG = 7
R2ROWS = 200
R3ROWS = 32

F32 = jnp.float32
BF16 = jnp.bfloat16


def split_np(table):
    hi = table.astype(np.float32).astype(ml_dtypes.bfloat16)
    lo = (table - hi.astype(np.float64)).astype(np.float32).astype(ml_dtypes.bfloat16)
    return hi, lo


def wave_tables():
    k = np.arange(KZ) - KZ // 2
    phase = np.mod(k[:, None] * np.arange(NC)[None, :], NC) * (2 * np.pi / NC)
    return np.cos(phase), np.sin(phase)


def interpolation_np():
    offset = np.arange(NF)[:, None] - 2 * np.arange(NC)[None, :]
    k = np.arange(1, NC // 2)
    phase = np.mod(offset[:, :, None] * k, NF) * (2 * np.pi / NF)
    return (1 + 2 * np.cos(phase).sum(2)) / NC


def tables():
    c, s = wave_tables()
    u = interpolation_np()
    w1 = np.zeros((2 * KZ, 384))
    for q in range(16):
        t, v = divmod(q, NG)
        at = 128 * t + 9 * v
        pl_ = slice(NP * q, NP * q + NP)
        w1[:KZ, at : at + NP] = c[:, pl_]
        w1[KZ:, at : at + NP] = -s[:, pl_]
        w1[:KZ, at + 64 : at + 64 + NP] = s[:, pl_]
        w1[KZ:, at + 64 : at + 64 + NP] = c[:, pl_]
    e2 = np.zeros((256, 512))
    e2[:KZ, :NC] = c
    e2[128 : 128 + KZ, :NC] = -s
    e2[:KZ, 256 : 256 + NC] = s
    e2[128 : 128 + KZ, 256 : 256 + NC] = c
    er = np.concatenate([np.concatenate([c.T, -s.T], 1), np.concatenate([s.T, c.T], 1)], 0)
    rows = np.array(
        [
            [9 * (16 * yh + 2 * z + core) + g for z in range(8) for yh in range(2) for g in range(9)]
            for core in range(2)
        ]
    )
    ug = u[rows]
    uf = np.zeros((NC, 384))
    for fb in range(8):
        t, v = divmod(fb, 3)
        uf[:, 128 * t + 36 * v : 128 * t + 36 * v + 36] = u[36 * fb : 36 * fb + 36].T
    uft = np.tile(uf[128:], (8, 1))
    return w1, e2, er, ug, uf[:128], uft, u.T


def fold(table, axis):
    hi, lo = split_np(table)
    return np.concatenate([hi, hi, lo], axis)


def split(x):
    hi = x.astype(BF16)
    return hi, (x - hi.astype(F32)).astype(BF16)


def dot(a, b):
    return jnp.dot(a, b, preferred_element_type=F32)


def dot3(a, b_hi, b_lo):
    hi, lo = split(a)
    return dot(hi, b_hi) + (dot(hi, b_lo) + dot(lo, b_hi))


def lanes(shape):
    return lax.broadcasted_iota(jnp.int32, shape, 1)


def k1_body(occ_ref, x_ref, col_ref, whi_ref, wlo_ref, o_ref, xs, ys):
    fft = lax.axis_index("x") * 2 + lax.axis_index("yl")
    col = col_ref[pl.ds(fft, 1), :]
    k0 = jnp.floor((col.astype(F32) + 0.5) * (1.0 / KZ)).astype(jnp.int32)
    k1 = col - k0 * KZ - KZ // 2
    k0 = k0 - KZ // 2
    k2 = lax.broadcasted_iota(jnp.int32, (KZ, CB), 0) - KZ // 2
    inside = k2 * k2 + (k0 * k0 + k1 * k1) <= R2
    xs[:, 640:768] = jnp.zeros((2 * KZ, 128), F32)
    xs[0:KZ, 0:CB] = jnp.where(inside, x_ref[0, 0], 0.0)
    xs[KZ : 2 * KZ, 0:CB] = jnp.where(inside, x_ref[0, 1], 0.0)
    for j in range(6):
        rows = 128 if j < 5 else 32
        xt = xs[:, 128 * j : 128 * j + 128].T[0:rows]
        ys[128 * j : 128 * j + rows, :] = dot3(xt, whi_ref[...], wlo_ref[...])
    weight = occ_ref[0].astype(F32) * (1.0 / BANDS)
    lane = lanes((GR, 128))
    for q in range(16):
        t, v = divmod(q, NG)
        acc = jnp.full((GR, 128), weight, F32)
        for g in range(NG):
            part = ys[GR * g : GR * g + GR, 128 * t : 128 * t + 128]
            if g != v:
                part = pltpu.roll(part, (9 * (g - v)) % 128, 1)
            half = lane & 63
            acc = jnp.where((half >= 9 * g) & (half < 9 * g + 9), part, acc)
        o_ref[q] = acc


def k2_body(row_ref, r_ref, ehi_ref, elo_ref, er_ref, ug_ref, keep_ref, send_ref, st, box, hs, gs):
    core = lax.axis_index("core")
    box[...] = jnp.zeros(box.shape, F32)
    lane = lanes((GR, 128)) & 63
    for fb in range(8):
        for g in range(NG):
            n = min(GR, CB - GR * g)
            first = r_ref[fb, 0:n, :]
            second = r_ref[8 + fb, 0:n, :]
            if g != 0:
                first = pltpu.roll(first, (-9 * g) % 128, 1)
            if g != 1:
                second = pltpu.roll(second, (9 - 9 * g) % 128, 1)
            st[CB * fb + GR * g : CB * fb + GR * g + n, :] = jnp.where(lane[0:n] < 9, first, second)

    def place(i, carry):
        for t in range(16):
            c = i * 16 + t
            box[pl.ds(row_ref[c], 1), :] = st[pl.ds(c, 1), :]
        return carry

    lax.fori_loop(0, NCOLS // 16, place, 0)

    def along_second(i, carry):
        parts = []
        for t in range(8):
            at = pl.multiple_of((i * 8 + t) * 128, 128)
            flipped = box[pl.ds(at, 128), :].T
            parts.append(jnp.concatenate([flipped[0:24], flipped[64:88]], 1))
        line = jnp.concatenate(parts, 0)
        half = dot3(line, ehi_ref[...], elo_ref[...])
        for j in range(4):
            hs[j, pl.ds(pl.multiple_of(i * 192, 192), 192), :] = half[:, 128 * j : 128 * j + 128]
        return carry

    lax.fori_loop(0, 9, along_second, 0)

    def plane(p, carry):
        density = None
        for b in range(2):
            half = [hs[j, pl.ds(9 * b + p, KZ, stride=24), :] for j in range(4)]
            rows = [jnp.concatenate(half[0:2], 1), jnp.concatenate(half[2:4], 1)]
            hi, lo = split(jnp.concatenate(rows, 0))
            full = dot(er_ref[...], jnp.concatenate([hi, lo, hi], 0))
            sq = full * full
            part = (sq[0:NC] + sq[NC : 2 * NC]) * r_ref[8 * b, 0:1, 63:64]
            density = part if density is None else density + part
        hi, lo = split(density)
        rhs = jnp.concatenate([hi, lo, hi], 0)
        gs[p, 0:NC, :] = dot(ug_ref[core], rhs)
        gs[p, NC : 2 * NC, :] = dot(ug_ref[1 - core], rhs)
        return carry

    lax.fori_loop(0, NP, plane, 0)
    tail_lane = lanes((18, 128))
    for part, out in enumerate((keep_ref, send_ref)):
        for z in range(8):
            at = NC * part + 18 * z
            tail = None
            for p in range(NP):
                out[z, 18 * p : 18 * p + 18, :] = gs[p, at : at + 18, 0:128]
                end = gs[p, at : at + 18, 128:256]
                if p == 8:
                    out[z, 180:198, :] = end
                elif p == 0:
                    tail = end
                else:
                    tail = jnp.where(tail_lane < 16 * p, tail, pltpu.roll(end, 16 * p, 1))
            out[z, 162:180, :] = tail


def k3_body(r_ref, fhi_ref, flo_ref, thi_ref, tlo_ref, o_ref, ss, ts, fs):
    total = r_ref[0]
    for z in range(1, 8):
        total = total + r_ref[z]
    ss[...] = total
    lane = lanes((18, 128))
    ts[160:168, :] = jnp.zeros((8, 128), F32)
    for p in range(NP):
        if p < 8:
            tail = jnp.where((lane >= 16 * p) & (lane < 16 * p + 16), ss[162:180, :], 0.0)
        else:
            tail = jnp.where(lane < 16, ss[180:198, :], 0.0)
        ts[18 * p : 18 * p + 18, :] = tail
    fine = dot3(ss[0:168, :], fhi_ref[...], flo_ref[...]) + dot3(
        ts[...], thi_ref[...], tlo_ref[...]
    )
    for t in range(3):
        fs[t] = fine[:, 128 * t : 128 * t + 128]
    lane = lanes((NP, 128))
    for yh in range(2):
        for fb in range(8):
            t, v = divmod(fb, 3)
            for b in range(3):
                acc = None
                for a in range(3):
                    part = fs[t, pl.ds(9 * yh + 3 * a + b, NP, stride=18), :]
                    if a != v:
                        part = pltpu.roll(part, (36 * (a - v)) % 128, 1)
                    acc = part if acc is None else jnp.where(lane < 36 * a, acc, part)
                o_ref[8 * yh + fb, 9 * b : 9 * b + 9, :] = acc


def k4_body(r_ref, uhi_ref, ulo_ref, o_ref, xs, ys):
    for b in range(3):
        for q in range(16):
            xs[b, 9 * q : 9 * q + 9, :] = r_ref[q, 9 * b : 9 * b + 9, :]
        ys[b] = dot3(xs[b].T, uhi_ref[...], ulo_ref[...])
        for a in range(3):
            o_ref[3 * a + b] = ys[b, 36 * a : 36 * a + 36, :]


def vmem(n):
    return [pl.BlockSpec(memory_space=pltpu.VMEM)] * n


def smem():
    return [pl.BlockSpec(memory_space=pltpu.SMEM)]


def call(body, name, in_specs, outs, scratch, flops):
    return pl.pallas_call(
        body,
        out_shape=outs,
        in_specs=in_specs,
        out_specs=jax.tree.map(lambda _: pl.BlockSpec(memory_space=pltpu.VMEM), outs),
        scratch_shapes=[pltpu.VMEM(s, F32) for s in scratch],
        name=name,
        cost_estimate=pl.CostEstimate(flops=flops, bytes_accessed=2_000_000, transcendentals=0),
    )


def shape(*dims):
    return jax.ShapeDtypeStruct(dims, F32)


def local(coefficients, col_index, occupation):
    w1, e2, er, ug, uf, uft, uh = tables()
    whi, wlo = split_np(w1)
    ehi, elo = split_np(e2)
    fhi, flo = split_np(uf)
    thi, tlo = split_np(uft)
    uhi, ulo = split_np(uh)
    columns = col_index.reshape(8, CB)
    rows = (col_index // KZ) * 128 + col_index % KZ
    sent = call(
        k1_body, "lines", smem() + vmem(4), shape(16, GR, 128), [(2 * KZ, 768), (NG * GR, 384)], 10**9
    )(occupation, coefficients, columns, whi, wlo)
    got = lax.all_to_all(sent, PLANE, split_axis=0, concat_axis=0, tiled=True)
    keep, send = call(
        k2_body,
        "planes",
        smem() + vmem(5),
        (shape(8, R2ROWS, 128), shape(8, R2ROWS, 128)),
        [(NCOLS, 128), (KZ * 128, 128), (4, KZ * 24, 128), (NP, NF, 256)],
        10**10,
    )(rows, got, ehi, elo, fold(er, 1), fold(ug, 2))
    keep = keep + lax.ppermute(send, "core", [(0, 1), (1, 0)])
    got = lax.all_to_all(keep, "z", split_axis=0, concat_axis=0, tiled=True)
    sent = call(
        k3_body,
        "second",
        vmem(5),
        shape(16, R3ROWS, 128),
        [(R2ROWS, 128), (168, 128), (3, 168, 128)],
        10**9,
    )(got, fhi, flo, thi, tlo)
    got = lax.all_to_all(sent, PLANE, split_axis=0, concat_axis=0, tiled=True)
    return call(
        k4_body, "third", vmem(3), shape(9, 36, NF), [(3, NC, 128), (3, 128, NF)], 10**9
    )(got, uhi, ulo)


def solution(mesh):
    axes = Mesh(mesh.devices.reshape(SIZES), AXES)
    band, fft = ("yh", "z", "core"), ("x", "yl")
    return jax.shard_map(
        local,
        mesh=axes,
        in_specs=(P(band, None, None, fft), P(), P(band)),
        out_specs=P(band, fft, None),
        check_vma=False,
    )
```

time: 305 us -> 102 us (0.33)
  the two profiles are of different devices: /device:TPU:32 before, /device:TPU:8 now
where the time goes in v1:
time: 102 us; the launch traced here: 101 us
  blocking collectives  45.2 us (44%)
  Pallas kernels  28.4 us (28%)
  waiting for transfers between devices  15.2 us (15%)
  starting transfers between devices  7.53 us (7%)
  local copies, waits for them, and re-layouts  2.31 us (2%)
  other arithmetic  1.87 us (2%)
    all_to_all x1, blocking collectives, local(): got = lax.all_to_all(keep, 'z', split_axis=0, concat_axis=0, tiled=True)  32.5 us
    pallas_call x1, Pallas kernels, local(): call(k2_body, 'planes', smem() + vmem(5), (shape(8, R2ROWS, 128), shape(8...  19.7 us
    all_to_all x1, blocking collectives, local(): got = lax.all_to_all(sent, PLANE, split_axis=0, concat_axis=0, tiled=True)  12.7 us
    all_to_all x1, waiting for transfers between devices, local(): got = lax.all_to_all(sent, PLANE, split_axis=0, concat_axis=0, tiled=True)  12.7 us
    all_to_all x1, starting transfers between devices, local(): got = lax.all_to_all(sent, PLANE, split_axis=0, concat_axis=0, tiled=True)  7.52 us
    pallas_call x1, Pallas kernels, local(): call(k1_body, 'lines', smem() + vmem(4), shape(16, GR, 128), [(2 * KZ, 76...  3.64 us
    pallas_call x1, Pallas kernels, local(): call(k3_body, 'second', vmem(5), shape(16, R3ROWS, 128), [(R2ROWS, 128),...  2.67 us
    ppermute x1, waiting for transfers between devices, local(): keep = keep + lax.ppermute(send, 'core', [(0, 1), (1, 0)])  2.54 us
  transfers between devices with their start and end apart: 2, of which 2 were waited for; matrix products, arithmetic and copies ran while one was open for 1% of the time, Pallas kernels for 0%

profile of v1, /device:TPU:8, one launch (start us, length us, event | category | flops | bytes accessed | tf_op | source)
XLA Modules:
  0.0 101.1 jit_solution(6437176033300592367)
XLA Ops:
  0.7 1.4 %reshape.3.col_ref = s32[8,648]{1,0:T(8,128)} reshape(s32[5184]{0:T(1024)} %param.16) | data formatting | bytes 41472 | tf_op jit(solution)/shard_map/reshape | solution.py:278
  2.1 3.6 %lines.1 = f32[16,96,128]{2,1,0:T(8,128)} custom-call(s32[1]{0:T(128)S(6)} %copy.16.occ_ref, f32[1,2,72,648]{3,2,1,0:T(8,128)} %x_ref.1, s32[8,648]{1,0:T(8,128)} %reshape.3.col_ref, bf16[144,384]{1,0:T(8,128)(2,1)} %constant.46.clone.whi_ref, bf16[144,384]{1,0:T(8,128)(2,1)} %constant.47.clone.wlo_ref), custom_call_target="tpu_custom_call" | custom-call | flops 1000000000 | bytes 2000000 | tf_op jit(solution)/shard_map/lines/pallas_call | solution.py:280
  5.7 0.0 copy-start.1
  5.7 7.5 %all-to-all-start = ((f32[16,96,128]{2,1,0:T(8,128)}), f32[16,96,128]{2,1,0:T(8,128)S(1)}, u32[]{:S(2)}, u32[]{:S(2)}) async-start(f32[16,96,128]{2,1,0:T(8,128)} %lines.1), calls=%async_computation | async-start | bytes 1572864 | tf_op jit(solution)/shard_map/all_to_all | solution.py:283
  13.3 0.0 copy-done.1
  13.3 0.6 fusion.1.row_ref
  13.9 12.7 %all-to-all-done.r_ref = f32[16,96,128]{2,1,0:T(8,128)S(1)} async-done(((f32[16,96,128]{2,1,0:T(8,128)}), f32[16,96,128]{2,1,0:T(8,128)S(1)}, u32[]{:S(2)}, u32[]{:S(2)}) %all-to-all-start) | async-done | bytes 786464 | tf_op jit(solution)/shard_map/all_to_all | solution.py:283
  26.6 0.0 copy-start
  26.6 0.9 copy-done
  27.5 19.7 %planes.1 = (f32[8,200,128]{2,1,0:T(8,128)}, f32[8,200,128]{2,1,0:T(8,128)}) custom-call(s32[5184]{0:T(1024)} %fusion.1.row_ref, f32[16,96,128]{2,1,0:T(8,128)} %copy-done, bf16[256,512]{1,0:T(8,128)(2,1)} %constant.48.clone.ehi_ref, bf16[256,512]{1,0:T(8,128)(2,1)} %constant.49.clone.elo_ref, bf16[288,432]{1,0:T(8,128)(2,1)} %constant.50.clone.er_ref, ...), custom_call_target="tpu_custom_call" | custom-call | flops 10000000000 | bytes 2000000 | tf_op jit(solution)/shard_map/planes/pallas_call | solution.py:284
  47.1 0.0 collective-permute-start
  47.1 2.5 %collective-permute-done = f32[8,200,128]{2,1,0:T(8,128)S(1)} collective-permute-done((f32[8,200,128]{2,1,0:T(8,128)}, f32[8,200,128]{2,1,0:T(8,128)S(1)}, u32[]{:S(2)}, u32[]{:S(2)}) %collective-permute-start) | collective-permute-done | bytes 819232 | tf_op jit(solution)/shard_map/ppermute | solution.py:292
  49.7 1.2 %add.15 = f32[8,200,128]{2,1,0:T(8,128)S(1)} add(f32[8,200,128]{2,1,0:T(8,128)} %get-tuple-element.7, f32[8,200,128]{2,1,0:T(8,128)S(1)} %collective-permute-done) | non-fusion elementwise | flops 204800 | bytes 2457600 | tf_op jit(solution)/shard_map/add | solution.py:292
  50.9 32.5 %all_to_all.15.r_ref = f32[8,200,128]{2,1,0:T(8,128)} all-to-all(f32[8,200,128]{2,1,0:T(8,128)S(1)} %add.15), channel_id=1, replica_groups=mesh['yh'=2,'z'=8,'core'=2,'x'=4,'yl'=2] {'z'}, dimensions={0} | all-to-all | bytes 1638400 | tf_op jit(solution)/shard_map/all_to_all | solution.py:293
  83.4 2.7 %second.1 = f32[16,32,128]{2,1,0:T(8,128)} custom-call(f32[8,200,128]{2,1,0:T(8,128)} %all_to_all.15.r_ref, bf16[128,384]{1,0:T(8,128)(2,1)} %constant.52.clone.fhi_ref, bf16[128,384]{1,0:T(8,128)(2,1)} %constant.53.clone.flo_ref, bf16[128,384]{1,0:T(8,128)(2,1)} %constant.54.clone.thi_ref, bf16[128,384]{1,0:T(8,128)(2,1)} %constant.55.clone.tlo_ref), custom_call_target="tpu_custom_call" | custom-call | flops 1000000000 | bytes 2000000 | tf_op jit(solution)/shard_map/second/pallas_call | solution.py:294
  86.1 12.7 %all_to_all.16.r_ref = f32[16,32,128]{2,1,0:T(8,128)} all-to-all(f32[16,32,128]{2,1,0:T(8,128)} %second.1), channel_id=1, replica_groups=mesh['yh'=2,'z'=8,'core'=2,'x'=4,'yl'=2] {'yh','x','yl'}, dimensions={0} | all-to-all | bytes 524288 | tf_op jit(solution)/shard_map/all_to_all | solution.py:302
  98.8 2.4 %third.1 = f32[9,36,288]{2,1,0:T(8,128)} custom-call(f32[16,32,128]{2,1,0:T(8,128)} %all_to_all.16.r_ref, bf16[144,288]{1,0:T(8,128)(2,1)} %constant.56.clone.uhi_ref, bf16[144,288]{1,0:T(8,128)(2,1)} %constant.57.clone.ulo_ref), custom_call_target="tpu_custom_call" | custom-call | flops 1000000000 | bytes 2000000 | tf_op jit(solution)/shard_map/third/pallas_call | solution.py:303
Async XLA Ops:
  5.7 7.5 %copy-start.1 = (s32[5184]{0:T(1024)S(1)}, s32[5184]{0:T(1024)}, u32[]{:S(2)}) copy-start(s32[5184]{0:T(1024)} %param.16) | copy-start | bytes 62212
  5.7 20.8 %all-to-all-start = ((f32[16,96,128]{2,1,0:T(8,128)}), f32[16,96,128]{2,1,0:T(8,128)S(1)}, u32[]{:S(2)}, u32[]{:S(2)}) async-start(f32[16,96,128]{2,1,0:T(8,128)} %lines.1), calls=%async_computation | async-start | bytes 1572864 | tf_op jit(solution)/shard_map/all_to_all | solution.py:283
  26.6 0.9 copy-start
  47.1 2.5 %collective-permute-start = (f32[8,200,128]{2,1,0:T(8,128)}, f32[8,200,128]{2,1,0:T(8,128)S(1)}, u32[]{:S(2)}, u32[]{:S(2)}) collective-permute-start(f32[8,200,128]{2,1,0:T(8,128)} %get-tuple-element.8), channel_id=1, source_target_pairs={{0,8},{8,0},{1,9},{9,1},{2,10},{10,2},{3,11},{11,3},{4,12},{12,4},... | collective-permute-start | bytes 2457608 | tf_op jit(solution)/shard_map/ppermute | solution.py:292

commit v2 on v1

v2 whole, which is shorter than its diff:
```python
import jax
import jax.numpy as jnp
import ml_dtypes
import numpy as np
from jax import lax
from jax.experimental import pallas as pl
from jax.experimental.pallas import tpu as pltpu
from jax.sharding import Mesh, PartitionSpec as P

NC = 144
NF = 288
KZ = 72
NCOLS = 5184
BANDS = 32
R2 = (KZ // 2) ** 2

AXES = ("yh", "zh", "zl", "core", "x", "yl")
SIZES = (2, 4, 2, 2, 4, 2)
BAND, FFT = ("yh", "zh", "zl", "core"), ("x", "yl")
PLANE = ("yh", "x", "yl", "zl")
ND = 32
NB = 4
NP = 5
NZ = ND * NP
CB = NCOLS // 8
GR = 56
NG = 12
R2ROWS = 216
R3ROWS = 16

F32 = jnp.float32
BF16 = jnp.bfloat16


def split_np(table):
    hi = table.astype(np.float32).astype(ml_dtypes.bfloat16)
    lo = (table - hi.astype(np.float64)).astype(np.float32).astype(ml_dtypes.bfloat16)
    return hi, lo


def wave_tables(points):
    k = np.arange(KZ) - KZ // 2
    phase = np.mod(k[:, None] * np.arange(points)[None, :], points) * (2 * np.pi / points)
    return np.cos(phase), np.sin(phase)


def interpolation_np(points):
    offset = np.arange(NF)[:, None] * points - NF * np.arange(points)[None, :]
    k = np.arange(1, NC // 2)
    phase = np.mod(offset[:, :, None] * k, NF * points) * (2 * np.pi / (NF * points))
    return (1 + 2 * np.cos(phase).sum(2)) / points


def tables():
    c, s = wave_tables(NZ)
    w1 = np.zeros((2 * KZ, 384))
    for q in range(ND):
        t, v = divmod(q, NG)
        at = 128 * t + NP * v
        own = slice(NP * q, NP * q + NP)
        w1[:KZ, at : at + NP] = c[:, own]
        w1[KZ:, at : at + NP] = -s[:, own]
        w1[:KZ, at + 64 : at + 64 + NP] = s[:, own]
        w1[KZ:, at + 64 : at + 64 + NP] = c[:, own]
    c, s = wave_tables(NC)
    e2 = np.zeros((256, 512))
    e2[:KZ, :NC] = c
    e2[128 : 128 + KZ, :NC] = -s
    e2[:KZ, 256 : 256 + NC] = s
    e2[128 : 128 + KZ, 256 : 256 + NC] = c
    er = np.concatenate([np.concatenate([c.T, -s.T], 1), np.concatenate([s.T, c.T], 1)], 0)
    u = interpolation_np(NC)
    rows = np.array(
        [
            [9 * (16 * yh + 2 * z + core) + g for z in range(8) for yh in range(2) for g in range(9)]
            for core in range(2)
        ]
    )
    ug = u[rows]
    uf = np.zeros((NC, 384))
    for fb in range(8):
        t, v = divmod(fb, 3)
        uf[:, 128 * t + 36 * v : 128 * t + 36 * v + 36] = u[36 * fb : 36 * fb + 36].T
    uft = np.tile(uf[128:], (8, 1))
    return w1, e2, er, ug, uf[:128], uft, interpolation_np(NZ).T


def fold(table, axis):
    hi, lo = split_np(table)
    return np.concatenate([hi, hi, lo], axis)


def split(x):
    hi = x.astype(BF16)
    return hi, (x - hi.astype(F32)).astype(BF16)


def dot(a, b):
    return jnp.dot(a, b, preferred_element_type=F32)


def dot3(a, b_hi, b_lo):
    hi, lo = split(a)
    return dot(hi, b_hi) + (dot(hi, b_lo) + dot(lo, b_hi))


def lanes(shape):
    return lax.broadcasted_iota(jnp.int32, shape, 1)


def k1_body(occ_ref, x_ref, col_ref, whi_ref, wlo_ref, o_ref, xs, ys):
    fft = lax.axis_index("x") * 2 + lax.axis_index("yl")
    col = col_ref[pl.ds(fft, 1), :]
    k0 = jnp.floor((col.astype(F32) + 0.5) * (1.0 / KZ)).astype(jnp.int32)
    k1 = col - k0 * KZ - KZ // 2
    k0 = k0 - KZ // 2
    k2 = lax.broadcasted_iota(jnp.int32, (KZ, CB), 0) - KZ // 2
    inside = k2 * k2 + (k0 * k0 + k1 * k1) <= R2
    xs[:, 640:768] = jnp.zeros((2 * KZ, 128), F32)
    xs[0:KZ, 0:CB] = jnp.where(inside, x_ref[0, 0], 0.0)
    xs[KZ : 2 * KZ, 0:CB] = jnp.where(inside, x_ref[0, 1], 0.0)
    for j in range(6):
        rows = 128 if j < 5 else 32
        xt = xs[:, 128 * j : 128 * j + 128].T[0:rows]
        ys[128 * j : 128 * j + rows, :] = dot3(xt, whi_ref[...], wlo_ref[...])
    weight = occ_ref[0].astype(F32) * (1.0 / BANDS)
    lane = lanes((GR, 128))
    for q in range(ND):
        t, v = divmod(q, NG)
        acc = jnp.full((GR, 128), weight, F32)
        for g in range(NG):
            part = ys[GR * g : GR * g + GR, 128 * t : 128 * t + 128]
            if g != v:
                part = pltpu.roll(part, (NP * (g - v)) % 128, 1)
            half = lane & 63
            acc = jnp.where((half >= NP * g) & (half < NP * g + NP), part, acc)
        o_ref[q] = acc


def k2_body(row_ref, r_ref, ehi_ref, elo_ref, er_ref, ug_ref, keep_ref, send_ref, st, box, hs, gs):
    core = lax.axis_index("core")
    box[...] = jnp.zeros(box.shape, F32)
    lane = lanes((GR, 128)) & 63
    for fb in range(8):
        for g in range(NG):
            n = min(GR, CB - GR * g)
            acc = None
            for b in range(NB):
                part = r_ref[source(b, fb), 0:n, :]
                if b != g:
                    part = pltpu.roll(part, (NP * (b - g)) % 128, 1)
                acc = part if acc is None else jnp.where(lane[0:n] < NP * b, acc, part)
            st[CB * fb + GR * g : CB * fb + GR * g + n, :] = acc

    def place(i, carry):
        for t in range(48):
            c = i * 48 + t
            box[pl.ds(row_ref[c], 1), :] = st[pl.ds(c, 1), :]
        return carry

    lax.fori_loop(0, NCOLS // 48, place, 0)

    def along_second(i, carry):
        parts = []
        for t in range(8):
            at = pl.multiple_of((i * 8 + t) * 128, 128)
            flipped = box[pl.ds(at, 128), :].T
            parts.append(jnp.concatenate([flipped[0:24], flipped[64:88]], 1))
        line = jnp.concatenate(parts, 0)
        half = dot3(line, ehi_ref[...], elo_ref[...])
        for j in range(4):
            hs[j, pl.ds(pl.multiple_of(i * 192, 192), 192), :] = half[:, 128 * j : 128 * j + 128]
        return carry

    lax.fori_loop(0, 9, along_second, 0)

    def plane(p, carry):
        density = None
        for b in range(NB):
            half = [hs[j, pl.ds(NP * b + p, KZ, stride=24), :] for j in range(4)]
            rows = [jnp.concatenate(half[0:2], 1), jnp.concatenate(half[2:4], 1)]
            hi, lo = split(jnp.concatenate(rows, 0))
            full = dot(er_ref[...], jnp.concatenate([hi, lo, hi], 0))
            sq = full * full
            part = (sq[0:NC] + sq[NC : 2 * NC]) * r_ref[source(b, 0), 0:1, 63:64]
            density = part if density is None else density + part
        hi, lo = split(density)
        rhs = jnp.concatenate([hi, lo, hi], 0)
        gs[p, 0:NC, :] = dot(ug_ref[core], rhs)
        gs[p, NC : 2 * NC, :] = dot(ug_ref[1 - core], rhs)
        return carry

    lax.fori_loop(0, NP, plane, 0)
    tail_lane = lanes((36, 128))
    for part, out in enumerate((keep_ref, send_ref)):
        for z in range(4):
            at = NC * part + 36 * z
            tail = None
            for p in range(NP):
                out[z, 36 * p : 36 * p + 36, :] = gs[p, at : at + 36, 0:128]
                end = gs[p, at : at + 36, 128:256]
                if p == 0:
                    tail = end
                else:
                    tail = jnp.where(tail_lane < 16 * p, tail, pltpu.roll(end, 16 * p, 1))
            out[z, 36 * NP : 36 * NP + 36, :] = tail


def source(b, fb):
    return 16 * (b // 2) + 2 * fb + b % 2


def k3_body(r_ref, fhi_ref, flo_ref, thi_ref, tlo_ref, o_ref, ss, ts, fs):
    ss[...] = (r_ref[0] + r_ref[1]) + (r_ref[2] + r_ref[3])
    lane = lanes((36, 128))
    ts[176:184, :] = jnp.zeros((8, 128), F32)
    for p in range(NP):
        own = (lane >= 16 * p) & (lane < 16 * p + 16)
        ts[36 * p : 36 * p + 36, :] = jnp.where(own, ss[36 * NP : 36 * NP + 36, :], 0.0)
    fine = dot3(ss[0:184, :], fhi_ref[...], flo_ref[...]) + dot3(
        ts[...], thi_ref[...], tlo_ref[...]
    )
    for t in range(3):
        fs[t] = fine[:, 128 * t : 128 * t + 128]
    lane = lanes((NP, 128))
    for yh in range(2):
        for zl in range(2):
            for fb in range(8):
                t, v = divmod(fb, 3)
                for b in range(3):
                    acc = None
                    for a in range(3):
                        first = 18 * zl + 9 * yh + 3 * a + b
                        part = fs[t, pl.ds(first, NP, stride=36), :]
                        if a != v:
                            part = pltpu.roll(part, (36 * (a - v)) % 128, 1)
                        acc = part if acc is None else jnp.where(lane < 36 * a, acc, part)
                    o_ref[16 * yh + 2 * fb + zl, NP * b : NP * b + NP, :] = acc


def k4_body(r_ref, uhi_ref, ulo_ref, o_ref, xs, ys):
    for b in range(3):
        for q in range(ND):
            xs[b, NP * q : NP * q + NP, :] = r_ref[q, NP * b : NP * b + NP, :]
        ys[b] = dot3(xs[b].T, uhi_ref[...], ulo_ref[...])
        for a in range(3):
            o_ref[3 * a + b] = ys[b, 36 * a : 36 * a + 36, :]


def vmem(n):
    return [pl.BlockSpec(memory_space=pltpu.VMEM)] * n


def smem():
    return [pl.BlockSpec(memory_space=pltpu.SMEM)]


def call(body, name, in_specs, outs, scratch, flops, mib=12):
    return pl.pallas_call(
        body,
        out_shape=outs,
        in_specs=in_specs,
        out_specs=jax.tree.map(lambda _: pl.BlockSpec(memory_space=pltpu.VMEM), outs),
        scratch_shapes=[pltpu.VMEM(s, F32) for s in scratch],
        name=name,
        compiler_params=pltpu.CompilerParams(vmem_limit_bytes=mib * 2**20),
        cost_estimate=pl.CostEstimate(flops=flops, bytes_accessed=2_000_000, transcendentals=0),
    )


def shape(*dims):
    return jax.ShapeDtypeStruct(dims, F32)


def local(coefficients, col_index, occupation):
    w1, e2, er, ug, uf, uft, uh = tables()
    whi, wlo = split_np(w1)
    ehi, elo = split_np(e2)
    fhi, flo = split_np(uf)
    thi, tlo = split_np(uft)
    uhi, ulo = split_np(uh)
    columns = col_index.reshape(8, CB)
    rows = (col_index // KZ) * 128 + col_index % KZ
    sent = call(
        k1_body, "lines", smem() + vmem(4), shape(ND, GR, 128), [(2 * KZ, 768), (NG * GR, 384)], 10**9
    )(occupation, coefficients, columns, whi, wlo)
    got = lax.all_to_all(sent, PLANE, split_axis=0, concat_axis=0, tiled=True)
    keep, send = call(
        k2_body,
        "planes",
        smem() + vmem(5),
        (shape(4, R2ROWS, 128), shape(4, R2ROWS, 128)),
        [(NCOLS, 128), (KZ * 128, 128), (4, KZ * 24, 128), (NP, NF, 256)],
        10**10,
        28,
    )(rows, got, ehi, elo, fold(er, 1), fold(ug, 2))
    keep = keep + lax.ppermute(send, "core", [(0, 1), (1, 0)])
    got = lax.all_to_all(keep, "zh", split_axis=0, concat_axis=0, tiled=True)
    sent = call(
        k3_body,
        "second",
        vmem(5),
        shape(ND, R3ROWS, 128),
        [(R2ROWS, 128), (184, 128), (3, 184, 128)],
        10**9,
    )(got, fhi, flo, thi, tlo)
    got = lax.all_to_all(sent, PLANE, split_axis=0, concat_axis=0, tiled=True)
    return call(
        k4_body, "third", vmem(3), shape(9, 36, NF), [(3, NZ, 128), (3, 128, NF)], 10**9
    )(got, uhi, ulo)


def solution(mesh):
    axes = Mesh(mesh.devices.reshape(SIZES), AXES)
    return jax.shard_map(
        local,
        mesh=axes,
        in_specs=(P(BAND, None, None, FFT), P(), P(BAND)),
        out_specs=P(BAND, FFT, None),
        check_vma=False,
    )
```

time: 102 us -> 89.1 us (0.87)
  the two profiles are of different devices: /device:TPU:8 before, /device:TPU:64 now
where the time goes in v2:
time: 89.1 us; the launch traced here: 87.5 us
  blocking collectives  33.3 us (37%)
  Pallas kernels  22.5 us (25%)
  waiting for transfers between devices  18.2 us (20%)
  starting transfers between devices  8.91 us (10%)
  local copies, waits for them, and re-layouts  3.68 us (4%)
    all_to_all x1, blocking collectives, local(): got = lax.all_to_all(keep, 'zh', split_axis=0, concat_axis=0, tiled=True)  20.6 us
    pallas_call x1, Pallas kernels, local(): call(k2_body, 'planes', smem() + vmem(5), (shape(4, R2ROWS, 128), shape(4...  16.5 us
    all_to_all x1, waiting for transfers between devices, local(): got = lax.all_to_all(sent, PLANE, split_axis=0, concat_axis=0, tiled=True)  16.4 us
    all_to_all x1, blocking collectives, local(): got = lax.all_to_all(sent, PLANE, split_axis=0, concat_axis=0, tiled=True)  12.7 us
    all_to_all x1, starting transfers between devices, local(): got = lax.all_to_all(sent, PLANE, split_axis=0, concat_axis=0, tiled=True)  8.82 us
    pallas_call x1, Pallas kernels, local(): call(k1_body, 'lines', smem() + vmem(4), shape(ND, GR, 128), [(2 * KZ, 76...  3.98 us
    unnamed x28, local copies, waits for them, and re-layouts  2.86 us
  transfers between devices with their start and end apart: 2, of which 2 were waited for; matrix products, arithmetic and copies ran while one was open for 0% of the time, Pallas kernels for 0%

profile of v2, /device:TPU:64, one launch (start us, length us, event | category | flops | bytes accessed | tf_op | source)
XLA Modules:
  0.0 87.5 jit_solution(646658086451331460)
XLA Ops:
  0.0 0.8 reshape.3.col_ref
  1.5 0.0 copy-start
  1.5 1.0 %copy-done = f32[1,2,72,648]{3,2,1,0:T(8,128)S(1)} copy-done((f32[1,2,72,648]{3,2,1,0:T(8,128)S(1)}, f32[1,2,72,648]{3,2,1,0:T(8,128)}, u32[]{:S(2)}) %copy-start) | copy-done | bytes 373272
  2.5 0.9 %copy-done.7 = bf16[144,384]{1,0:T(8,128)(2,1)S(1)} copy-done((bf16[144,384]{1,0:T(8,128)(2,1)S(1)}, bf16[144,384]{1,0:T(8,128)(2,1)}, u32[]{:S(2)}) %copy-start.7) | copy-done | bytes 110616
  3.4 0.9 %copy-done.8 = bf16[144,384]{1,0:T(8,128)(2,1)S(1)} copy-done((bf16[144,384]{1,0:T(8,128)(2,1)S(1)}, bf16[144,384]{1,0:T(8,128)(2,1)}, u32[]{:S(2)}) %copy-start.8) | copy-done | bytes 110616
  4.3 4.0 %lines.1 = f32[32,56,128]{2,1,0:T(8,128)} custom-call(s32[1]{0:T(128)S(6)} %copy.16.occ_ref, f32[1,2,72,648]{3,2,1,0:T(8,128)S(1)} %copy-done, s32[8,648]{1,0:T(8,128)S(1)} %reshape.3.col_ref, bf16[144,384]{1,0:T(8,128)(2,1)S(1)} %copy-done.7, bf16[144,384]{1,0:T(8,128)(2,1)S(1)} %copy-done.8), custom_call_target="tpu_custom_call" | custom-call | flops 1000000000 | bytes 2000000 | tf_op jit(solution)/shard_map/lines/pallas_call | solution.py:284
  8.3 0.0 copy-start.4
  8.3 8.8 %all-to-all-start = ((f32[32,56,128]{2,1,0:T(8,128)}), f32[32,56,128]{2,1,0:T(8,128)S(1)}, u32[]{:S(2)}, u32[]{:S(2)}) async-start(f32[32,56,128]{2,1,0:T(8,128)} %lines.1), calls=%async_computation | async-start | bytes 1835008 | tf_op jit(solution)/shard_map/all_to_all | solution.py:287
  17.1 0.0 copy-done.13
  17.2 16.4 %all-to-all-done.r_ref = f32[32,56,128]{2,1,0:T(8,128)S(1)} async-done(((f32[32,56,128]{2,1,0:T(8,128)}), f32[32,56,128]{2,1,0:T(8,128)S(1)}, u32[]{:S(2)}, u32[]{:S(2)}) %all-to-all-start) | async-done | bytes 917536 | tf_op jit(solution)/shard_map/all_to_all | solution.py:287
  33.6 0.0 copy-done.1
  33.6 0.0 copy-done.2
  33.6 0.0 copy-done.3
  33.6 0.0 copy-done.4
  33.6 16.5 %planes.1 = (f32[4,216,128]{2,1,0:T(8,128)S(1)}, f32[4,216,128]{2,1,0:T(8,128)S(1)}) custom-call(s32[5184]{0:T(1024)S(1)} %fusion.1.row_ref, f32[32,56,128]{2,1,0:T(8,128)S(1)} %all-to-all-done.r_ref, bf16[256,512]{1,0:T(8,128)(2,1)S(1)} %copy-done.3, bf16[256,512]{1,0:T(8,128)(2,1)S(1)} %copy-done.4, bf16[288,432]{1,0:T(8,128)(2,1)S(1)} %copy-done.1, ...), custom_call_target="tpu_custom_call" | custom-call | flops 10000000000 | bytes 2000000 | tf_op jit(solution)/shard_map/planes/pallas_call | solution.py:288
  50.1 0.1 collective-permute-start
  50.2 1.8 %collective-permute-done = f32[4,216,128]{2,1,0:T(8,128)S(1)} collective-permute-done((f32[4,216,128]{2,1,0:T(8,128)S(1)}, f32[4,216,128]{2,1,0:T(8,128)S(1)}, u32[]{:S(2)}, u32[]{:S(2)}) %collective-permute-start) | collective-permute-done | bytes 442400 | tf_op jit(solution)/shard_map/ppermute | solution.py:297
  52.0 0.1 add.15
  52.1 0.0 copy-start.9
  52.1 0.0 copy-start.10
  52.1 0.0 copy-start.11
  52.1 0.0 copy-start.12
  52.1 20.6 %all_to_all.15.r_ref = f32[4,216,128]{2,1,0:T(8,128)S(1)} all-to-all(f32[4,216,128]{2,1,0:T(8,128)S(1)} %add.15), channel_id=1, replica_groups=mesh['yh'=2,'zh'=4,'zl'=2,'core'=2,'x'=4,'yl'=2] {'zh'}, dimensions={0} | all-to-all | bytes 884736 | tf_op jit(solution)/shard_map/all_to_all | solution.py:298
  72.8 0.0 copy-done.9
  72.8 0.0 copy-done.10
  72.8 0.0 copy-done.11
  72.8 0.6 second.1
  73.4 0.0 copy-start.5
  73.4 0.0 copy-start.6
  73.4 12.7 %all_to_all.16.r_ref = f32[32,16,128]{2,1,0:T(8,128)S(1)} all-to-all(f32[32,16,128]{2,1,0:T(8,128)S(1)} %second.1), channel_id=1, replica_groups=mesh['yh'=2,'zh'=4,'zl'=2,'core'=2,'x'=4,'yl'=2] {'yh','x','yl','zl'}, dimensions={0} | all-to-all | bytes 524288 | tf_op jit(solution)/shard_map/all_to_all | solution.py:307
  86.2 0.0 copy-done.6
  86.2 1.4 %third.1 = f32[9,36,288]{2,1,0:T(8,128)} custom-call(f32[32,16,128]{2,1,0:T(8,128)S(1)} %all_to_all.16.r_ref, bf16[160,288]{1,0:T(8,128)(2,1)S(1)} %copy-done.5, bf16[160,288]{1,0:T(8,128)(2,1)S(1)} %copy-done.6), custom_call_target="tpu_custom_call" | custom-call | flops 1000000000 | bytes 2000000 | tf_op jit(solution)/shard_map/third/pallas_call | solution.py:308
  (9 shorter events, 0.0 us)
Async XLA Ops:
  1.5 1.0 %copy-start = (f32[1,2,72,648]{3,2,1,0:T(8,128)S(1)}, f32[1,2,72,648]{3,2,1,0:T(8,128)}, u32[]{:S(2)}) copy-start(f32[1,2,72,648]{3,2,1,0:T(8,128)} %x_ref.1) | copy-start | bytes 1119748
  2.5 0.9 %copy-start.7 = (bf16[144,384]{1,0:T(8,128)(2,1)S(1)}, bf16[144,384]{1,0:T(8,128)(2,1)}, u32[]{:S(2)}) copy-start(bf16[144,384]{1,0:T(8,128)(2,1)} %constant.46.clone.whi_ref) | copy-start | bytes 331780
  3.4 0.9 %copy-start.8 = (bf16[144,384]{1,0:T(8,128)(2,1)S(1)}, bf16[144,384]{1,0:T(8,128)(2,1)}, u32[]{:S(2)}) copy-start(bf16[144,384]{1,0:T(8,128)(2,1)} %constant.47.clone.wlo_ref) | copy-start | bytes 331780
  8.3 8.9 %copy-start.13 = (s32[5184]{0:T(1024)S(1)}, s32[5184]{0:T(1024)}, u32[]{:S(2)}) copy-start(s32[5184]{0:T(1024)} %param.16) | copy-start | bytes 62212
  8.3 25.3 %copy-start.1 = (bf16[288,432]{1,0:T(8,128)(2,1)S(1)}, bf16[288,432]{1,0:T(8,128)(2,1)}, u32[]{:S(2)}) copy-start(bf16[288,432]{1,0:T(8,128)(2,1)} %constant.50.clone.er_ref) | copy-start | bytes 746500
  8.3 25.3 %copy-start.2 = (bf16[2,144,432]{2,1,0:T(8,128)(2,1)S(1)}, bf16[2,144,432]{2,1,0:T(8,128)(2,1)}, u32[]{:S(2)}) copy-start(bf16[2,144,432]{2,1,0:T(8,128)(2,1)} %constant.51.clone.ug_ref) | copy-start | bytes 746500
  8.3 25.3 %copy-start.3 = (bf16[256,512]{1,0:T(8,128)(2,1)S(1)}, bf16[256,512]{1,0:T(8,128)(2,1)}, u32[]{:S(2)}) copy-start(bf16[256,512]{1,0:T(8,128)(2,1)} %constant.48.clone.ehi_ref) | copy-start | bytes 786436
  8.3 25.3 %copy-start.4 = (bf16[256,512]{1,0:T(8,128)(2,1)S(1)}, bf16[256,512]{1,0:T(8,128)(2,1)}, u32[]{:S(2)}) copy-start(bf16[256,512]{1,0:T(8,128)(2,1)} %constant.49.clone.elo_ref) | copy-start | bytes 786436
  8.3 25.3 %all-to-all-start = ((f32[32,56,128]{2,1,0:T(8,128)}), f32[32,56,128]{2,1,0:T(8,128)S(1)}, u32[]{:S(2)}, u32[]{:S(2)}) async-start(f32[32,56,128]{2,1,0:T(8,128)} %lines.1), calls=%async_computation | async-start | bytes 1835008 | tf_op jit(solution)/shard_map/all_to_all | solution.py:287
  50.1 1.9 %collective-permute-start = (f32[4,216,128]{2,1,0:T(8,128)S(1)}, f32[4,216,128]{2,1,0:T(8,128)S(1)}, u32[]{:S(2)}, u32[]{:S(2)}) collective-permute-start(f32[4,216,128]{2,1,0:T(8,128)S(1)} %get-tuple-element.8), channel_id=1, source_target_pairs={{0,8},{8,0},{1,9},{9,1},{2,10},{10,2},{3,11},{11,3},{4,12},{12,4},... | collective-permute-start | bytes 1327112 | tf_op jit(solution)/shard_map/ppermute | solution.py:297
  52.1 20.7 %copy-start.9 = (bf16[128,384]{1,0:T(8,128)(2,1)S(1)}, bf16[128,384]{1,0:T(8,128)(2,1)}, u32[]{:S(2)}) copy-start(bf16[128,384]{1,0:T(8,128)(2,1)} %constant.52.clone.fhi_ref) | copy-start | bytes 294916
  52.1 20.7 %copy-start.10 = (bf16[128,384]{1,0:T(8,128)(2,1)S(1)}, bf16[128,384]{1,0:T(8,128)(2,1)}, u32[]{:S(2)}) copy-start(bf16[128,384]{1,0:T(8,128)(2,1)} %constant.53.clone.flo_ref) | copy-start | bytes 294916
  52.1 20.6 %copy-start.11 = (bf16[128,384]{1,0:T(8,128)(2,1)S(1)}, bf16[128,384]{1,0:T(8,128)(2,1)}, u32[]{:S(2)}) copy-start(bf16[128,384]{1,0:T(8,128)(2,1)} %constant.54.clone.thi_ref) | copy-start | bytes 294916
  52.1 20.6 %copy-start.12 = (bf16[128,384]{1,0:T(8,128)(2,1)S(1)}, bf16[128,384]{1,0:T(8,128)(2,1)}, u32[]{:S(2)}) copy-start(bf16[128,384]{1,0:T(8,128)(2,1)} %constant.55.clone.tlo_ref) | copy-start | bytes 294916
  73.4 12.7 %copy-start.5 = (bf16[160,288]{1,0:T(8,128)(2,1)S(1)}, bf16[160,288]{1,0:T(8,128)(2,1)}, u32[]{:S(2)}) copy-start(bf16[160,288]{1,0:T(8,128)(2,1)} %constant.56.clone.uhi_ref) | copy-start | bytes 276484
  73.4 12.7 %copy-start.6 = (bf16[160,288]{1,0:T(8,128)(2,1)S(1)}, bf16[160,288]{1,0:T(8,128)(2,1)}, u32[]{:S(2)}) copy-start(bf16[160,288]{1,0:T(8,128)(2,1)} %constant.57.clone.ulo_ref) | copy-start | bytes 276484

commit v3 on v2

--- a/solution.py
+++ b/solution.py
@@ -23,8 +23,7 @@
 NP = 5
 NZ = ND * NP
 CB = NCOLS // 8
-GR = 56
-NG = 12
+R1ROWS = 56
 R2ROWS = 216
 R3ROWS = 16
 
@@ -53,15 +52,7 @@
 
 def tables():
     c, s = wave_tables(NZ)
-    w1 = np.zeros((2 * KZ, 384))
-    for q in range(ND):
-        t, v = divmod(q, NG)
-        at = 128 * t + NP * v
-        own = slice(NP * q, NP * q + NP)
-        w1[:KZ, at : at + NP] = c[:, own]
-        w1[KZ:, at : at + NP] = -s[:, own]
-        w1[:KZ, at + 64 : at + 64 + NP] = s[:, own]
-        w1[KZ:, at + 64 : at + 64 + NP] = c[:, own]
+    w1 = np.concatenate([np.concatenate([c.T, -s.T], 1), np.concatenate([s.T, c.T], 1)], 0)
     c, s = wave_tables(NC)
     e2 = np.zeros((256, 512))
     e2[:KZ, :NC] = c
@@ -70,13 +61,14 @@
     e2[128 : 128 + KZ, 256 : 256 + NC] = c
     er = np.concatenate([np.concatenate([c.T, -s.T], 1), np.concatenate([s.T, c.T], 1)], 0)
     u = interpolation_np(NC)
-    rows = np.array(
-        [
-            [9 * (16 * yh + 2 * z + core) + g for z in range(8) for yh in range(2) for g in range(9)]
-            for core in range(2)
-        ]
-    )
-    ug = u[rows]
+    ug = np.zeros((2, 4, 40, NC))
+    for core in range(2):
+        for z in range(8):
+            for yh in range(2):
+                at = 18 * (z % 2) + 9 * yh
+                first = 9 * (16 * yh + 2 * z + core)
+                ug[core, z // 2, at : at + 9] = u[first : first + 9]
+    ug = ug.reshape(2, 160, NC)
     uf = np.zeros((NC, 384))
     for fb in range(8):
         t, v = divmod(fb, 3)
@@ -108,7 +100,14 @@
     return lax.broadcasted_iota(jnp.int32, shape, 1)
 
 
-def k1_body(occ_ref, x_ref, col_ref, whi_ref, wlo_ref, o_ref, xs, ys):
+def k1_body(occ_hbm, x_hbm, col_ref, w_hbm, o_ref, occ_ref, xr, wv, xs, ys, sems):
+    copies = [
+        pltpu.make_async_copy(occ_hbm, occ_ref, sems.at[0]),
+        pltpu.make_async_copy(x_hbm.at[0], xr, sems.at[1]),
+        pltpu.make_async_copy(w_hbm, wv, sems.at[2]),
+    ]
+    for copy in copies:
+        copy.start()
     fft = lax.axis_index("x") * 2 + lax.axis_index("yl")
     col = col_ref[pl.ds(fft, 1), :]
     k0 = jnp.floor((col.astype(F32) + 0.5) * (1.0 / KZ)).astype(jnp.int32)
@@ -117,40 +116,52 @@
     k2 = lax.broadcasted_iota(jnp.int32, (KZ, CB), 0) - KZ // 2
     inside = k2 * k2 + (k0 * k0 + k1 * k1) <= R2
     xs[:, 640:768] = jnp.zeros((2 * KZ, 128), F32)
-    xs[0:KZ, 0:CB] = jnp.where(inside, x_ref[0, 0], 0.0)
-    xs[KZ : 2 * KZ, 0:CB] = jnp.where(inside, x_ref[0, 1], 0.0)
-    for j in range(6):
-        rows = 128 if j < 5 else 32
-        xt = xs[:, 128 * j : 128 * j + 128].T[0:rows]
-        ys[128 * j : 128 * j + rows, :] = dot3(xt, whi_ref[...], wlo_ref[...])
-    weight = occ_ref[0].astype(F32) * (1.0 / BANDS)
-    lane = lanes((GR, 128))
+    for copy in copies:
+        copy.wait()
+    xs[0:KZ, 0:CB] = jnp.where(inside, xr[0], 0.0)
+    xs[KZ : 2 * KZ, 0:CB] = jnp.where(inside, xr[1], 0.0)
+    for n in range(3):
+        hi, lo = split(xs[:, 256 * n : 256 * n + 256])
+        y = dot(wv[...], jnp.concatenate([hi, lo, hi], 0))
+        ys[2 * n] = y[:, 0:128]
+        ys[2 * n + 1] = y[:, 128:256]
+    lane = lanes((NZ, 128))
+    ys[5, 0:NZ, :] = jnp.where(lane < 8, ys[5, 0:NZ, :], pltpu.roll(ys[5, NZ : 2 * NZ, :], 8, 1))
+    weight = jnp.full((1, 128), occ_ref[0].astype(F32) * (1.0 / BANDS), F32)
     for q in range(ND):
-        t, v = divmod(q, NG)
-        acc = jnp.full((GR, 128), weight, F32)
-        for g in range(NG):
-            part = ys[GR * g : GR * g + GR, 128 * t : 128 * t + 128]
-            if g != v:
-                part = pltpu.roll(part, (NP * (g - v)) % 128, 1)
-            half = lane & 63
-            acc = jnp.where((half >= NP * g) & (half < NP * g + NP), part, acc)
-        o_ref[q] = acc
-
-
-def k2_body(row_ref, r_ref, ehi_ref, elo_ref, er_ref, ug_ref, keep_ref, send_ref, st, box, hs, gs):
+        for j in range(6):
+            for ri in range(2 if j < 5 else 1):
+                at, own = 10 * j + NP * ri, NZ * ri + NP * q
+                o_ref[q, at : at + NP, :] = ys[j, own : own + NP, :]
+        o_ref[q, 55:56, :] = weight
+
+
+def source(b, fb):
+    return 16 * (b // 2) + 2 * fb + b % 2
+
+
+def k2_body(row_ref, r_ref, ehi_ref, elo_ref, er_ref, ug_ref, *rest):
+    keep2, keep0, keep1, keep3, send2, send_rest, tr, st, box, hs, gs = rest
     core = lax.axis_index("core")
-    box[...] = jnp.zeros(box.shape, F32)
-    lane = lanes((GR, 128)) & 63
-    for fb in range(8):
-        for g in range(NG):
-            n = min(GR, CB - GR * g)
-            acc = None
+    zh = lax.axis_index("zh")
+    box[NCOLS : NCOLS + 56, :] = jnp.zeros((56, 128), F32)
+
+    def unpack(fb, carry):
+        base = pl.multiple_of(fb * CB, 8)
+        for j in range(6):
             for b in range(NB):
-                part = r_ref[source(b, fb), 0:n, :]
-                if b != g:
-                    part = pltpu.roll(part, (NP * (b - g)) % 128, 1)
-                acc = part if acc is None else jnp.where(lane[0:n] < NP * b, acc, part)
-            st[CB * fb + GR * g : CB * fb + GR * g + n, :] = acc
+                for ri in range(2 if j < 5 else 1):
+                    at = 24 * ri + NP * b
+                    own = 10 * j + NP * ri
+                    tr[j, at : at + NP, :] = r_ref[source(b, fb), own : own + NP, :]
+            if j < 5:
+                st[pl.ds(pl.multiple_of(base + 128 * j, 8), 128), 0:48] = tr[j].T
+            else:
+                tr[5, 24:48, :] = pltpu.roll(tr[5, 0:24, :], 120, 1)
+                st[pl.ds(pl.multiple_of(base + 640, 8), 8), 0:48] = tr[5].T[0:8]
+        return carry
+
+    lax.fori_loop(0, 8, unpack, 0)
 
     def place(i, carry):
         for t in range(48):
@@ -163,9 +174,9 @@
     def along_second(i, carry):
         parts = []
         for t in range(8):
-            at = pl.multiple_of((i * 8 + t) * 128, 128)
+            at = pl.multiple_of((i * 8 + t) * KZ, 8)
             flipped = box[pl.ds(at, 128), :].T
-            parts.append(jnp.concatenate([flipped[0:24], flipped[64:88]], 1))
+            parts.append(jnp.concatenate([flipped[0:24], flipped[24:48]], 1))
         line = jnp.concatenate(parts, 0)
         half = dot3(line, ehi_ref[...], elo_ref[...])
         for j in range(4):
@@ -182,36 +193,33 @@
             hi, lo = split(jnp.concatenate(rows, 0))
             full = dot(er_ref[...], jnp.concatenate([hi, lo, hi], 0))
             sq = full * full
-            part = (sq[0:NC] + sq[NC : 2 * NC]) * r_ref[source(b, 0), 0:1, 63:64]
+            part = (sq[0:NC] + sq[NC : 2 * NC]) * r_ref[source(b, 0), 55:56, 0:1]
             density = part if density is None else density + part
         hi, lo = split(density)
         rhs = jnp.concatenate([hi, lo, hi], 0)
-        gs[p, 0:NC, :] = dot(ug_ref[core], rhs)
-        gs[p, NC : 2 * NC, :] = dot(ug_ref[1 - core], rhs)
+        gs[p, 0] = dot(ug_ref[core], rhs).reshape(4, 40, 256)
+        gs[p, 1] = dot(ug_ref[1 - core], rhs).reshape(4, 40, 256)
         return carry
 
     lax.fori_loop(0, NP, plane, 0)
     tail_lane = lanes((36, 128))
-    for part, out in enumerate((keep_ref, send_ref)):
-        for z in range(4):
-            at = NC * part + 36 * z
+    sends = [send_rest.at[0], send_rest.at[1], send2, send_rest.at[2]]
+    for part, outs in enumerate(((keep0, keep1, keep2, keep3), sends)):
+        for d in range(4):
+            z = (zh + d) & 3
             tail = None
             for p in range(NP):
-                out[z, 36 * p : 36 * p + 36, :] = gs[p, at : at + 36, 0:128]
-                end = gs[p, at : at + 36, 128:256]
+                outs[d][36 * p : 36 * p + 36, :] = gs[p, part, z, 0:36, 0:128]
+                end = gs[p, part, z, 0:36, 128:256]
                 if p == 0:
                     tail = end
                 else:
                     tail = jnp.where(tail_lane < 16 * p, tail, pltpu.roll(end, 16 * p, 1))
-            out[z, 36 * NP : 36 * NP + 36, :] = tail
-
-
-def source(b, fb):
-    return 16 * (b // 2) + 2 * fb + b % 2
-
-
-def k3_body(r_ref, fhi_ref, flo_ref, thi_ref, tlo_ref, o_ref, ss, ts, fs):
-    ss[...] = (r_ref[0] + r_ref[1]) + (r_ref[2] + r_ref[3])
+            outs[d][36 * NP : 36 * NP + 36, :] = tail
+
+
+def k3_body(r0_ref, r1_ref, r2_ref, fhi_ref, flo_ref, thi_ref, tlo_ref, o_ref, ss, ts, fs):
+    ss[...] = r0_ref[...] + (r1_ref[...] + r2_ref[...])
     lane = lanes((36, 128))
     ts[176:184, :] = jnp.zeros((8, 128), F32)
     for p in range(NP):
@@ -261,7 +269,7 @@
         out_shape=outs,
         in_specs=in_specs,
         out_specs=jax.tree.map(lambda _: pl.BlockSpec(memory_space=pltpu.VMEM), outs),
-        scratch_shapes=[pltpu.VMEM(s, F32) for s in scratch],
+        scratch_shapes=[pltpu.VMEM(s, F32) if isinstance(s, tuple) else s for s in scratch],
         name=name,
         compiler_params=pltpu.CompilerParams(vmem_limit_bytes=mib * 2**20),
         cost_estimate=pl.CostEstimate(flops=flops, bytes_accessed=2_000_000, transcendentals=0),
@@ -274,36 +282,65 @@
 
 def local(coefficients, col_index, occupation):
     w1, e2, er, ug, uf, uft, uh = tables()
-    whi, wlo = split_np(w1)
     ehi, elo = split_np(e2)
     fhi, flo = split_np(uf)
     thi, tlo = split_np(uft)
     uhi, ulo = split_np(uh)
     columns = col_index.reshape(8, CB)
-    rows = (col_index // KZ) * 128 + col_index % KZ
+    hbm = pl.BlockSpec(memory_space=pltpu.HBM)
     sent = call(
-        k1_body, "lines", smem() + vmem(4), shape(ND, GR, 128), [(2 * KZ, 768), (NG * GR, 384)], 10**9
-    )(occupation, coefficients, columns, whi, wlo)
+        k1_body,
+        "lines",
+        [hbm, hbm] + vmem(1) + [hbm],
+        shape(ND, R1ROWS, 128),
+        [
+            pltpu.SMEM((1,), jnp.int32),
+            (2, KZ, CB),
+            pltpu.VMEM((2 * NZ, 6 * KZ), BF16),
+            (2 * KZ, 768),
+            (6, 2 * NZ, 128),
+            pltpu.SemaphoreType.DMA((3,)),
+        ],
+        10**9,
+    )(occupation, coefficients, columns, fold(w1, 1))
     got = lax.all_to_all(sent, PLANE, split_axis=0, concat_axis=0, tiled=True)
-    keep, send = call(
+    block = shape(R2ROWS, 128)
+    keep2, keep0, keep1, keep3, send2, send_rest = call(
         k2_body,
         "planes",
         smem() + vmem(5),
-        (shape(4, R2ROWS, 128), shape(4, R2ROWS, 128)),
-        [(NCOLS, 128), (KZ * 128, 128), (4, KZ * 24, 128), (NP, NF, 256)],
+        (block, block, block, block, block, shape(3, R2ROWS, 128)),
+        [
+            (6, 48, 128),
+            (NCOLS, 128),
+            (NCOLS + 56, 128),
+            (4, KZ * 24, 128),
+            (NP, 2, 4, 40, 256),
+        ],
         10**10,
-        28,
-    )(rows, got, ehi, elo, fold(er, 1), fold(ug, 2))
-    keep = keep + lax.ppermute(send, "core", [(0, 1), (1, 0)])
-    got = lax.all_to_all(keep, "zh", split_axis=0, concat_axis=0, tiled=True)
+        24,
+    )(col_index, got, ehi, elo, fold(er, 1), fold(ug, 2))
+    swap = [(0, 1), (1, 0)]
+    up = [(i, (i + 1) % 4) for i in range(4)]
+    down = [(i, (i - 1) % 4) for i in range(4)]
+    keep2 = keep2 + lax.ppermute(send2, "core", swap)
+    rest = lax.ppermute(send_rest, "core", swap)
+    from_below = lax.ppermute(keep2[:104], "zh", up)
+    from_above = lax.ppermute(keep2[104:], "zh", down)
+    keep1 = keep1 + rest[1]
+    keep3 = keep3 + rest[2]
+    keep1 = jnp.concatenate([keep1[:104] + from_below, keep1[104:]], 0)
+    keep3 = jnp.concatenate([keep3[:104], keep3[104:] + from_above], 0)
+    from_below = lax.ppermute(keep1, "zh", up)
+    from_above = lax.ppermute(keep3, "zh", down)
     sent = call(
         k3_body,
         "second",
-        vmem(5),
+        vmem(7),
         shape(ND, R3ROWS, 128),
         [(R2ROWS, 128), (184, 128), (3, 184, 128)],
         10**9,
-    )(got, fhi, flo, thi, tlo)
+    )(keep0 + rest[0], from_below, from_above, fhi, flo, thi, tlo)
     got = lax.all_to_all(sent, PLANE, split_axis=0, concat_axis=0, tiled=True)
     return call(
         k4_body, "third", vmem(3), shape(9, 36, NF), [(3, NZ, 128), (3, 128, NF)], 10**9

time: 89.1 us -> 81 us (0.909); the launches traced: 87.5 us -> 80.6 us
  waiting for transfers between devices: 18.2 us -> 12.2 us
  blocking collectives: 33.3 us -> 37.6 us
  Pallas kernels: 22.5 us -> 18.4 us
    all_to_all x1 -> x2, blocking collectives: 12.7 us -> 37.6 us  [local(): got = lax.all_to_all(sent, PLANE, split_axis=0, concat_axis=0, tiled=True)]
    all_to_all x1 -> x0, blocking collectives: 20.6 us -> none  [local(): got = lax.all_to_all(keep, 'zh', split_axis=0, concat_axis=0, tiled=True)]
    all_to_all x1 -> x0, waiting for transfers between devices: 16.4 us -> none  [local(): got = lax.all_to_all(sent, PLANE, split_axis=0, concat_axis=0, tiled=True)]
    ppermute x1 -> x6, waiting for transfers between devices: 1.78 us -> 12.2 us  [the longest x1 6.24 us: local(): from_above = lax.ppermute(keep3, 'zh', down)]
    all_to_all x1 -> x0, starting transfers between devices: 8.82 us -> none  [local(): got = lax.all_to_all(sent, PLANE, split_axis=0, concat_axis=0, tiled=True)]
    ppermute x1 -> x6, starting transfers between devices: 0.09 us -> 8.49 us  [the longest x1 4.15 us: local(): from_below = lax.ppermute(keep1, 'zh', up)]
    pallas_call x3, Pallas kernels: 21.1 us -> 17 us  [the longest x1 15.2 us: local(): call(k2_body, 'planes', smem() + vmem(5), (block, block, block, block, bl...]
    unnamed x28 -> x26, local copies, waits for them, and re-layouts: 2.86 us -> 2.06 us
  transfers between devices with their start and end apart: 2 -> 6, of which waited for: 2 -> 5; matrix products, arithmetic and copies ran while one was open for 0% -> 0% of each run, Pallas kernels for 0% -> 0%
where the time goes in v3:
time: 81 us; the launch traced here: 80.6 us
  blocking collectives  37.6 us (46%)
  Pallas kernels  18.4 us (23%)
  waiting for transfers between devices  12.2 us (15%)
  starting transfers between devices  8.49 us (10%)
  local copies, waits for them, and re-layouts  2.9 us (4%)
  between operations  0.89 us (1%)
    all_to_all x2, blocking collectives, local(): got = lax.all_to_all(sent, PLANE, split_axis=0, concat_axis=0, tiled=True)  37.6 us
    pallas_call x1, Pallas kernels, local(): call(k2_body, 'planes', smem() + vmem(5), (block, block, block, block, bl...  15.2 us
    ppermute x1, waiting for transfers between devices, local(): from_above = lax.ppermute(keep3, 'zh', down)  6.24 us
    ppermute x1, starting transfers between devices, local(): from_below = lax.ppermute(keep1, 'zh', up)  4.15 us
    ppermute x1, starting transfers between devices, local(): from_below = lax.ppermute(keep2[:104], 'zh', up)  3.66 us
    ppermute x1, waiting for transfers between devices, local(): from_below = lax.ppermute(keep2[:104], 'zh', up)  2.12 us
    unnamed x26, local copies, waits for them, and re-layouts  2.06 us
    ppermute x1, waiting for transfers between devices, local(): from_below = lax.ppermute(keep1, 'zh', up)  2.01 us
  transfers between devices with their start and end apart: 6, of which 5 were waited for; matrix products, arithmetic and copies ran while one was open for 0% of the time, Pallas kernels for 0%

profile of v3, /device:TPU:64, one launch (start us, length us, event | category | flops | bytes accessed | tf_op | source)
XLA Modules:
  0.0 80.6 jit_solution(8948495047111796399)
XLA Ops:
  0.7 0.8 %reshape.3.col_ref = s32[8,648]{1,0:T(8,128)S(1)} reshape(s32[5184]{0:T(1024)} %row_ref.1) | data formatting | bytes 41472 | tf_op jit(solution)/shard_map/reshape | solution.py:289
  1.5 0.0 copy-start.1
  1.5 1.0 %copy-done.1 = f32[1,2,72,648]{3,2,1,0:T(8,128)S(1)} copy-done((f32[1,2,72,648]{3,2,1,0:T(8,128)S(1)}, f32[1,2,72,648]{3,2,1,0:T(8,128)}, u32[]{:S(2)}) %copy-start.1) | copy-done | bytes 373272
  2.5 1.0 %copy-done.3 = bf16[320,432]{1,0:T(8,128)(2,1)S(1)} copy-done((bf16[320,432]{1,0:T(8,128)(2,1)S(1)}, bf16[320,432]{1,0:T(8,128)(2,1)}, u32[]{:S(2)}) %copy-start.3) | copy-done | bytes 276504
  3.5 1.2 %lines.1 = f32[32,56,128]{2,1,0:T(8,128)S(1)} custom-call(s32[1]{0:T(128)S(6)} %copy.15.occ_hbm, f32[1,2,72,648]{3,2,1,0:T(8,128)S(1)} %copy-done.1, s32[8,648]{1,0:T(8,128)S(1)} %reshape.3.col_ref, bf16[320,432]{1,0:T(8,128)(2,1)S(1)} %copy-done.3), custom_call_target="tpu_custom_call" | custom-call | flops 1000000000 | bytes 2000000 | tf_op jit(solution)/shard_map/lines/pallas_call | solution.py:291
  4.6 0.0 copy-start
  4.6 0.0 copy-start.2
  4.7 0.0 copy-start.4
  4.7 0.0 copy-start.5
  4.7 0.0 copy-start.6
  4.7 25.1 %all_to_all.10.r_ref = f32[32,56,128]{2,1,0:T(8,128)S(1)} all-to-all(f32[32,56,128]{2,1,0:T(8,128)S(1)} %lines.1), channel_id=1, replica_groups=mesh['yh'=2,'zh'=4,'zl'=2,'core'=2,'x'=4,'yl'=2] {'yh','x','yl','zl'}, dimensions={0} | all-to-all | bytes 1835008 | tf_op jit(solution)/shard_map/all_to_all | solution.py:306
  29.8 15.2 %planes.1 = (f32[216,128]{1,0:T(8,128)S(1)}, f32[216,128]{1,0:T(8,128)S(1)}, f32[216,128]{1,0:T(8,128)S(1)}, f32[216,128]{1,0:T(8,128)S(1)}, f32[216,128]{1,0:T(8,128)S(1)}, /*index=5*/f32[3,216,128]{2,1,0:T(8,128)S(1)}) custom-call(s32[5184]{0:T(1024)S(1)} %copy-done, f32[32,56,128]{2,1,0:T(8,128)S(1)} %all_to_all.10.r_ref, bf16[256,512]{1,0:T(8,128)(2,1)S(1)} %copy-done.6, ...), custom_call_target="tpu_custom_call" | custom-call | flops 10000000000 | bytes 2000000 | tf_op jit(solution)/shard_map/planes/pallas_call | solution.py:308
  45.0 0.1 collective-permute-start
  45.1 0.5 collective-permute-start.1
  45.6 1.3 %collective-permute-done.1 = f32[216,128]{1,0:T(8,128)S(1)} collective-permute-done((f32[216,128]{1,0:T(8,128)S(1)}, f32[216,128]{1,0:T(8,128)S(1)}, u32[]{:S(2)}, u32[]{:S(2)}) %collective-permute-start.1) | collective-permute-done | bytes 110624 | tf_op jit(solution)/shard_map/ppermute | solution.py:326
  46.9 3.7 %collective-permute-start.2 = (f32[104,128]{1,0:T(8,128)S(1)}, f32[104,128]{1,0:T(8,128)S(1)}, u32[]{:S(2)}, u32[]{:S(2)}) collective-permute-start(f32[104,128]{1,0:T(8,128)S(1)} %slice.39), channel_id=1, source_target_pairs={{0,32},{32,64},{64,96},{96,0},{1,33},{33,65},{65,97},{97,1},{2,34}... | collective-permute-start | bytes 159752 | tf_op jit(solution)/shard_map/ppermute | solution.py:328
  50.6 0.1 fusion
  50.7 2.1 %collective-permute-done.2 = f32[104,128]{1,0:T(8,128)S(1)} collective-permute-done((f32[104,128]{1,0:T(8,128)S(1)}, f32[104,128]{1,0:T(8,128)S(1)}, u32[]{:S(2)}, u32[]{:S(2)}) %collective-permute-start.2) | collective-permute-done | bytes 53280 | tf_op jit(solution)/shard_map/ppermute | solution.py:328
  52.8 0.0 copy-start.11
  52.8 0.0 copy-start.12
  52.9 4.2 %collective-permute-start.3 = (f32[216,128]{1,0:T(8,128)S(1)}, f32[216,128]{1,0:T(8,128)S(1)}, u32[]{:S(2)}, u32[]{:S(2)}) collective-permute-start(f32[216,128]{1,0:T(8,128)S(1)} %pad_maximum_fusion), channel_id=1, source_target_pairs={{0,32},{32,64},{64,96},{96,0},{1,33},{33,65},{65,97},{97,1},{2,34}... | collective-permute-start | bytes 331784 | tf_op jit(solution)/shard_map/ppermute | solution.py:334
  57.0 0.6 collective-permute-done.4
  57.6 0.0 copy-start.9
  57.6 0.0 copy-start.10
  57.7 0.1 collective-permute-start.5
  57.8 2.0 %collective-permute-done.3.r1_ref = f32[216,128]{1,0:T(8,128)S(1)} collective-permute-done((f32[216,128]{1,0:T(8,128)S(1)}, f32[216,128]{1,0:T(8,128)S(1)}, u32[]{:S(2)}, u32[]{:S(2)}) %collective-permute-start.3) | collective-permute-done | bytes 110624 | tf_op jit(solution)/shard_map/ppermute | solution.py:334
  59.8 6.2 %collective-permute-done.5.r2_ref = f32[216,128]{1,0:T(8,128)S(1)} collective-permute-done((f32[216,128]{1,0:T(8,128)S(1)}, f32[216,128]{1,0:T(8,128)S(1)}, u32[]{:S(2)}, u32[]{:S(2)}) %collective-permute-start.5) | collective-permute-done | bytes 110624 | tf_op jit(solution)/shard_map/ppermute | solution.py:335
  66.0 0.7 second.1
  66.7 0.0 copy-start.7
  66.7 0.0 copy-start.8
  66.7 12.5 %all_to_all.11.r_ref = f32[32,16,128]{2,1,0:T(8,128)S(1)} all-to-all(f32[32,16,128]{2,1,0:T(8,128)S(1)} %second.1), channel_id=1, replica_groups=mesh['yh'=2,'zh'=4,'zl'=2,'core'=2,'x'=4,'yl'=2] {'yh','x','yl','zl'}, dimensions={0} | all-to-all | bytes 524288 | tf_op jit(solution)/shard_map/all_to_all | solution.py:344
  79.3 1.4 %third.1 = f32[9,36,288]{2,1,0:T(8,128)} custom-call(f32[32,16,128]{2,1,0:T(8,128)S(1)} %all_to_all.11.r_ref, bf16[160,288]{1,0:T(8,128)(2,1)S(1)} %copy-done.8, bf16[160,288]{1,0:T(8,128)(2,1)S(1)} %copy-done.7), custom_call_target="tpu_custom_call" | custom-call | flops 1000000000 | bytes 2000000 | tf_op jit(solution)/shard_map/third/pallas_call | solution.py:345
  (23 shorter events, 0.1 us)
Async XLA Ops:
  1.5 1.0 %copy-start.1 = (f32[1,2,72,648]{3,2,1,0:T(8,128)S(1)}, f32[1,2,72,648]{3,2,1,0:T(8,128)}, u32[]{:S(2)}) copy-start(f32[1,2,72,648]{3,2,1,0:T(8,128)} %x_hbm.1) | copy-start | bytes 1119748
  2.5 1.0 %copy-start.3 = (bf16[320,432]{1,0:T(8,128)(2,1)S(1)}, bf16[320,432]{1,0:T(8,128)(2,1)}, u32[]{:S(2)}) copy-start(bf16[320,432]{1,0:T(8,128)(2,1)} %constant.22.clone.w_hbm) | copy-start | bytes 829444
  4.6 25.1 %copy-start = (s32[5184]{0:T(1024)S(1)}, s32[5184]{0:T(1024)}, u32[]{:S(2)}) copy-start(s32[5184]{0:T(1024)} %row_ref.1) | copy-start | bytes 62212
  4.6 25.1 %copy-start.2 = (bf16[2,160,432]{2,1,0:T(8,128)(2,1)S(1)}, bf16[2,160,432]{2,1,0:T(8,128)(2,1)}, u32[]{:S(2)}) copy-start(bf16[2,160,432]{2,1,0:T(8,128)(2,1)} %constant.26.clone.ug_ref) | copy-start | bytes 829444
  4.7 25.1 %copy-start.4 = (bf16[288,432]{1,0:T(8,128)(2,1)S(1)}, bf16[288,432]{1,0:T(8,128)(2,1)}, u32[]{:S(2)}) copy-start(bf16[288,432]{1,0:T(8,128)(2,1)} %constant.25.clone.er_ref) | copy-start | bytes 746500
  4.7 25.1 %copy-start.5 = (bf16[256,512]{1,0:T(8,128)(2,1)S(1)}, bf16[256,512]{1,0:T(8,128)(2,1)}, u32[]{:S(2)}) copy-start(bf16[256,512]{1,0:T(8,128)(2,1)} %constant.24.clone.elo_ref) | copy-start | bytes 786436
  4.7 25.1 %copy-start.6 = (bf16[256,512]{1,0:T(8,128)(2,1)S(1)}, bf16[256,512]{1,0:T(8,128)(2,1)}, u32[]{:S(2)}) copy-start(bf16[256,512]{1,0:T(8,128)(2,1)} %constant.23.clone.ehi_ref) | copy-start | bytes 786436
  45.0 5.6 %collective-permute-start = (f32[3,216,128]{2,1,0:T(8,128)S(1)}, f32[3,216,128]{2,1,0:T(8,128)S(1)}, u32[]{:S(2)}, u32[]{:S(2)}) collective-permute-start(f32[3,216,128]{2,1,0:T(8,128)S(1)} %get-tuple-element.12), channel_id=1, source_target_pairs={{0,8},{8,0},{1,9},{9,1},{2,10},{10,2},{3,11},{11,3},{4,12},{12,4},... | collective-permute-start | bytes 995336 | tf_op jit(solution)/shard_map/ppermute | solution.py:327
  45.1 1.8 %collective-permute-start.1 = (f32[216,128]{1,0:T(8,128)S(1)}, f32[216,128]{1,0:T(8,128)S(1)}, u32[]{:S(2)}, u32[]{:S(2)}) collective-permute-start(f32[216,128]{1,0:T(8,128)S(1)} %get-tuple-element.15), channel_id=1, source_target_pairs={{0,8},{8,0},{1,9},{9,1},{2,10},{10,2},{3,11},{11,3},{4,12},{12,4},... | collective-permute-start | bytes 331784 | tf_op jit(solution)/shard_map/ppermute | solution.py:326
  46.9 5.9 %collective-permute-start.2 = (f32[104,128]{1,0:T(8,128)S(1)}, f32[104,128]{1,0:T(8,128)S(1)}, u32[]{:S(2)}, u32[]{:S(2)}) collective-permute-start(f32[104,128]{1,0:T(8,128)S(1)} %slice.39), channel_id=1, source_target_pairs={{0,32},{32,64},{64,96},{96,0},{1,33},{33,65},{65,97},{97,1},{2,34}... | collective-permute-start | bytes 159752 | tf_op jit(solution)/shard_map/ppermute | solution.py:328
  50.6 7.0 %collective-permute-start.4 = (f32[112,128]{1,0:T(8,128)S(1)}, f32[112,128]{1,0:T(8,128)S(1)}, u32[]{:S(2)}, u32[]{:S(2)}) collective-permute-start(f32[112,128]{1,0:T(8,128)S(1)} %slice.44), channel_id=1, source_target_pairs={{0,96},{32,0},{64,32},{96,64},{1,97},{33,1},{65,33},{97,65},{2,98}... | collective-permute-start | bytes 172040 | tf_op jit(solution)/shard_map/ppermute | solution.py:329
  52.8 13.2 %copy-start.11 = (bf16[128,384]{1,0:T(8,128)(2,1)S(1)}, bf16[128,384]{1,0:T(8,128)(2,1)}, u32[]{:S(2)}) copy-start(bf16[128,384]{1,0:T(8,128)(2,1)} %constant.28.clone.flo_ref) | copy-start | bytes 294916
  52.8 13.2 %copy-start.12 = (bf16[128,384]{1,0:T(8,128)(2,1)S(1)}, bf16[128,384]{1,0:T(8,128)(2,1)}, u32[]{:S(2)}) copy-start(bf16[128,384]{1,0:T(8,128)(2,1)} %constant.27.clone.fhi_ref) | copy-start | bytes 294916
  52.9 6.9 %collective-permute-start.3 = (f32[216,128]{1,0:T(8,128)S(1)}, f32[216,128]{1,0:T(8,128)S(1)}, u32[]{:S(2)}, u32[]{:S(2)}) collective-permute-start(f32[216,128]{1,0:T(8,128)S(1)} %pad_maximum_fusion), channel_id=1, source_target_pairs={{0,32},{32,64},{64,96},{96,0},{1,33},{33,65},{65,97},{97,1},{2,34}... | collective-permute-start | bytes 331784 | tf_op jit(solution)/shard_map/ppermute | solution.py:334
  57.6 8.4 %copy-start.9 = (bf16[128,384]{1,0:T(8,128)(2,1)S(1)}, bf16[128,384]{1,0:T(8,128)(2,1)}, u32[]{:S(2)}) copy-start(bf16[128,384]{1,0:T(8,128)(2,1)} %constant.30.clone.tlo_ref) | copy-start | bytes 294916
  57.6 8.4 %copy-start.10 = (bf16[128,384]{1,0:T(8,128)(2,1)S(1)}, bf16[128,384]{1,0:T(8,128)(2,1)}, u32[]{:S(2)}) copy-start(bf16[128,384]{1,0:T(8,128)(2,1)} %constant.29.clone.thi_ref) | copy-start | bytes 294916
  57.7 8.3 %collective-permute-start.5 = (f32[216,128]{1,0:T(8,128)S(1)}, f32[216,128]{1,0:T(8,128)S(1)}, u32[]{:S(2)}, u32[]{:S(2)}) collective-permute-start(f32[216,128]{1,0:T(8,128)S(1)} %pad_maximum_fusion.1), channel_id=1, source_target_pairs={{0,96},{32,0},{64,32},{96,64},{1,97},{33,1},{65,33},{97,65},{2,98}... | collective-permute-start | bytes 331784 | tf_op jit(solution)/shard_map/ppermute | solution.py:335
  66.7 12.6 %copy-start.7 = (bf16[160,288]{1,0:T(8,128)(2,1)S(1)}, bf16[160,288]{1,0:T(8,128)(2,1)}, u32[]{:S(2)}) copy-start(bf16[160,288]{1,0:T(8,128)(2,1)} %constant.32.clone.ulo_ref) | copy-start | bytes 276484
  66.7 12.6 %copy-start.8 = (bf16[160,288]{1,0:T(8,128)(2,1)S(1)}, bf16[160,288]{1,0:T(8,128)(2,1)}, u32[]{:S(2)}) copy-start(bf16[160,288]{1,0:T(8,128)(2,1)} %constant.31.clone.uhi_ref) | copy-start | bytes 276484

commit v4 on v3

--- a/solution.py
+++ b/solution.py
@@ -54,11 +54,12 @@
     c, s = wave_tables(NZ)
     w1 = np.concatenate([np.concatenate([c.T, -s.T], 1), np.concatenate([s.T, c.T], 1)], 0)
     c, s = wave_tables(NC)
-    e2 = np.zeros((256, 512))
-    e2[:KZ, :NC] = c
-    e2[128 : 128 + KZ, :NC] = -s
-    e2[:KZ, 256 : 256 + NC] = s
-    e2[128 : 128 + KZ, 256 : 256 + NC] = c
+    e2 = np.zeros((256, 384))
+    for ri, (on_re, on_im) in enumerate(((c, -s), (s, c))):
+        for at, own in ((128 * ri, slice(0, 128)), (256 + 16 * ri, slice(128, NC))):
+            width = own.stop - own.start
+            e2[:KZ, at : at + width] = on_re[:, own]
+            e2[128 : 128 + KZ, at : at + width] = on_im[:, own]
     er = np.concatenate([np.concatenate([c.T, -s.T], 1), np.concatenate([s.T, c.T], 1)], 0)
     u = interpolation_np(NC)
     ug = np.zeros((2, 4, 40, NC))
@@ -100,29 +101,10 @@
     return lax.broadcasted_iota(jnp.int32, shape, 1)
 
 
-def k1_body(occ_hbm, x_hbm, col_ref, w_hbm, o_ref, occ_ref, xr, wv, xs, ys, sems):
-    copies = [
-        pltpu.make_async_copy(occ_hbm, occ_ref, sems.at[0]),
-        pltpu.make_async_copy(x_hbm.at[0], xr, sems.at[1]),
-        pltpu.make_async_copy(w_hbm, wv, sems.at[2]),
-    ]
-    for copy in copies:
-        copy.start()
-    fft = lax.axis_index("x") * 2 + lax.axis_index("yl")
-    col = col_ref[pl.ds(fft, 1), :]
-    k0 = jnp.floor((col.astype(F32) + 0.5) * (1.0 / KZ)).astype(jnp.int32)
-    k1 = col - k0 * KZ - KZ // 2
-    k0 = k0 - KZ // 2
-    k2 = lax.broadcasted_iota(jnp.int32, (KZ, CB), 0) - KZ // 2
-    inside = k2 * k2 + (k0 * k0 + k1 * k1) <= R2
-    xs[:, 640:768] = jnp.zeros((2 * KZ, 128), F32)
-    for copy in copies:
-        copy.wait()
-    xs[0:KZ, 0:CB] = jnp.where(inside, xr[0], 0.0)
-    xs[KZ : 2 * KZ, 0:CB] = jnp.where(inside, xr[1], 0.0)
+def k1_body(occ_ref, x_ref, w_ref, o_ref, ys):
     for n in range(3):
-        hi, lo = split(xs[:, 256 * n : 256 * n + 256])
-        y = dot(wv[...], jnp.concatenate([hi, lo, hi], 0))
+        hi, lo = split(x_ref[:, 256 * n : 256 * n + 256])
+        y = dot(w_ref[...], jnp.concatenate([hi, lo, hi], 0))
         ys[2 * n] = y[:, 0:128]
         ys[2 * n + 1] = y[:, 128:256]
     lane = lanes((NZ, 128))
@@ -141,67 +123,90 @@
 
 
 def k2_body(row_ref, r_ref, ehi_ref, elo_ref, er_ref, ug_ref, *rest):
-    keep2, keep0, keep1, keep3, send2, send_rest, tr, st, box, hs, gs = rest
+    keep2, keep0, keep1, keep3, send2, send_rest, tr, st, box, hs, gs, col_ref, sem = rest
+    columns = pltpu.make_async_copy(row_ref, col_ref, sem)
+    columns.start()
     core = lax.axis_index("core")
     zh = lax.axis_index("zh")
     box[NCOLS : NCOLS + 56, :] = jnp.zeros((56, 128), F32)
 
     def unpack(fb, carry):
-        base = pl.multiple_of(fb * CB, 8)
+        base = fb * CB
         for j in range(6):
             for b in range(NB):
                 for ri in range(2 if j < 5 else 1):
                     at = 24 * ri + NP * b
                     own = 10 * j + NP * ri
-                    tr[j, at : at + NP, :] = r_ref[source(b, fb), own : own + NP, :]
+                    tr[6 * fb + j, at : at + NP, :] = r_ref[source(b, fb), own : own + NP, :]
             if j < 5:
-                st[pl.ds(pl.multiple_of(base + 128 * j, 8), 128), 0:48] = tr[j].T
+                st[pl.ds(base + 128 * j, 128), 0:48] = tr[6 * fb + j].T
             else:
-                tr[5, 24:48, :] = pltpu.roll(tr[5, 0:24, :], 120, 1)
-                st[pl.ds(pl.multiple_of(base + 640, 8), 8), 0:48] = tr[5].T[0:8]
+                tr[6 * fb + 5, 24:48, :] = pltpu.roll(tr[6 * fb + 5, 0:24, :], 120, 1)
+                st[pl.ds(base + 640, 8), 0:48] = tr[6 * fb + 5].T[0:8]
         return carry
 
-    lax.fori_loop(0, 8, unpack, 0)
+    for fb in range(8):
+        unpack(fb, 0)
+    columns.wait()
 
     def place(i, carry):
-        for t in range(48):
-            c = i * 48 + t
-            box[pl.ds(row_ref[c], 1), :] = st[pl.ds(c, 1), :]
+        for t in range(216):
+            c = i * 216 + t
+            box[pl.ds(col_ref[c], 1), :] = st[pl.ds(c, 1), :]
         return carry
 
-    lax.fori_loop(0, NCOLS // 48, place, 0)
+    lax.fori_loop(0, NCOLS // 216, place, 0)
 
     def along_second(i, carry):
         parts = []
-        for t in range(8):
-            at = pl.multiple_of((i * 8 + t) * KZ, 8)
+        for t in range(36):
+            at = pl.multiple_of((i * 36 + t) * KZ, 8)
             flipped = box[pl.ds(at, 128), :].T
             parts.append(jnp.concatenate([flipped[0:24], flipped[24:48]], 1))
         line = jnp.concatenate(parts, 0)
         half = dot3(line, ehi_ref[...], elo_ref[...])
-        for j in range(4):
-            hs[j, pl.ds(pl.multiple_of(i * 192, 192), 192), :] = half[:, 128 * j : 128 * j + 128]
+        for j in range(3):
+            hs[j, pl.ds(pl.multiple_of(i * 864, 8), 864), :] = half[:, 128 * j : 128 * j + 128]
         return carry
 
-    lax.fori_loop(0, 9, along_second, 0)
+    lax.fori_loop(0, 2, along_second, 0)
+
+    lane = lanes((NC, 128))
+
+    def transformed(field):
+        hi, lo = split(field)
+        full = dot(er_ref[...], jnp.concatenate([hi, lo, hi], 0))
+        sq = full * full
+        return sq[0:NC] + sq[NC : 2 * NC]
 
     def plane(p, carry):
+        weight = [r_ref[source(b, 0), 55:56, 0:1] for b in range(NB)]
+        mains, tail, factor = [], None, None
+        for b in range(NB):
+            re, im, end = [hs[j, pl.ds(NP * b + p, KZ, stride=24), :] for j in range(3)]
+            mains.append(jnp.concatenate([re, im], 0))
+            re = pltpu.roll(end, 16 * b, 1) if b else end
+            im = pltpu.roll(end, 16 * b - 16, 1) if b > 1 else end if b else pltpu.roll(end, 112, 1)
+            end = jnp.concatenate([re, im], 0)
+            tail = jnp.where(lane < 16 * b, tail, end) if b else end
+            factor = jnp.where(lane < 16 * b, factor, weight[b]) if b else weight[b]
         density = None
-        for b in range(NB):
-            half = [hs[j, pl.ds(NP * b + p, KZ, stride=24), :] for j in range(4)]
-            rows = [jnp.concatenate(half[0:2], 1), jnp.concatenate(half[2:4], 1)]
-            hi, lo = split(jnp.concatenate(rows, 0))
-            full = dot(er_ref[...], jnp.concatenate([hi, lo, hi], 0))
-            sq = full * full
-            part = (sq[0:NC] + sq[NC : 2 * NC]) * r_ref[source(b, 0), 55:56, 0:1]
-            density = part if density is None else density + part
+        for b in range(0, NB, 2):
+            pair = transformed(jnp.concatenate(mains[b : b + 2], 1))
+            pair = pair[:, 0:128] * weight[b] + pair[:, 128:256] * weight[b + 1]
+            density = pair if density is None else density + pair
+        tail = transformed(tail) * factor
+        tail = tail + pltpu.roll(tail, 96, 1)
+        tail = tail + pltpu.roll(tail, 112, 1)
+        density = jnp.concatenate([density, tail], 1)
         hi, lo = split(density)
         rhs = jnp.concatenate([hi, lo, hi], 0)
         gs[p, 0] = dot(ug_ref[core], rhs).reshape(4, 40, 256)
         gs[p, 1] = dot(ug_ref[1 - core], rhs).reshape(4, 40, 256)
         return carry
 
-    lax.fori_loop(0, NP, plane, 0)
+    for p in range(NP):
+        plane(p, 0)
     tail_lane = lanes((36, 128))
     sends = [send_rest.at[0], send_rest.at[1], send2, send_rest.at[2]]
     for part, outs in enumerate(((keep0, keep1, keep2, keep3), sends)):
@@ -286,36 +291,37 @@
     fhi, flo = split_np(uf)
     thi, tlo = split_np(uft)
     uhi, ulo = split_np(uh)
-    columns = col_index.reshape(8, CB)
-    hbm = pl.BlockSpec(memory_space=pltpu.HBM)
+    fft = lax.axis_index("x") * 2 + lax.axis_index("yl")
+    columns = lax.dynamic_slice_in_dim(col_index, fft * CB, CB)
+    k0 = columns // KZ - KZ // 2
+    k1 = columns % KZ - KZ // 2
+    k2 = jnp.arange(KZ, dtype=jnp.int32) - KZ // 2
+    inside = (k0 * k0 + k1 * k1)[None, :] + (k2 * k2)[:, None] <= R2
+    masked = jnp.where(inside, coefficients[0], 0.0).reshape(2 * KZ, CB)
+    masked = jnp.pad(masked, ((0, 0), (0, 768 - CB)))
     sent = call(
         k1_body,
         "lines",
-        [hbm, hbm] + vmem(1) + [hbm],
+        smem() + vmem(2),
         shape(ND, R1ROWS, 128),
-        [
-            pltpu.SMEM((1,), jnp.int32),
-            (2, KZ, CB),
-            pltpu.VMEM((2 * NZ, 6 * KZ), BF16),
-            (2 * KZ, 768),
-            (6, 2 * NZ, 128),
-            pltpu.SemaphoreType.DMA((3,)),
-        ],
+        [(6, 2 * NZ, 128)],
         10**9,
-    )(occupation, coefficients, columns, fold(w1, 1))
+    )(occupation, masked, fold(w1, 1))
     got = lax.all_to_all(sent, PLANE, split_axis=0, concat_axis=0, tiled=True)
     block = shape(R2ROWS, 128)
     keep2, keep0, keep1, keep3, send2, send_rest = call(
         k2_body,
         "planes",
-        smem() + vmem(5),
+        [pl.BlockSpec(memory_space=pl.ANY)] + vmem(5),
         (block, block, block, block, block, shape(3, R2ROWS, 128)),
         [
-            (6, 48, 128),
+            (48, 48, 128),
             (NCOLS, 128),
             (NCOLS + 56, 128),
-            (4, KZ * 24, 128),
+            (3, KZ * 24, 128),
             (NP, 2, 4, 40, 256),
+            pltpu.SMEM((NCOLS,), jnp.int32),
+            pltpu.SemaphoreType.DMA,
         ],
         10**10,
         24,

time: 81 us -> 75.6 us (0.933)
  Pallas kernels: 18.4 us -> 13.5 us
  local copies, waits for them, and re-layouts: 2.9 us -> 1.12 us
  other arithmetic: 0.11 us -> 1.37 us
    pallas_call x2, Pallas kernels: 16.3 us -> 11.5 us  [the longest x1 10.9 us: local(): call(k2_body, 'planes', [pl.BlockSpec(memory_space=pl.ANY)] + vmem(5), (b...]
    select_n x0 -> x1, other arithmetic: none -> 1.06 us  [local(): masked = jnp.where(inside, coefficients[0], 0.0).reshape(2 * KZ, CB)]
    unnamed x26 -> x24, local copies, waits for them, and re-layouts: 2.06 us -> 1.07 us
    reshape x1 -> x0, local copies, waits for them, and re-layouts: 0.82 us -> none  [local(): columns = col_index.reshape(8, CB)]
where the time goes in v4:
time: 75.6 us; the launch traced here: 75.3 us
  blocking collectives  37.6 us (50%)
  Pallas kernels  13.5 us (18%)
  waiting for transfers between devices  12.2 us (16%)
  starting transfers between devices  8.5 us (11%)
  other arithmetic  1.37 us (2%)
  local copies, waits for them, and re-layouts  1.12 us (1%)
  between operations  0.89 us (1%)
    all_to_all x2, blocking collectives, local(): got = lax.all_to_all(sent, PLANE, split_axis=0, concat_axis=0, tiled=True)  37.6 us
    pallas_call x1, Pallas kernels, local(): call(k2_body, 'planes', [pl.BlockSpec(memory_space=pl.ANY)] + vmem(5), (b...  10.9 us
    ppermute x1, waiting for transfers between devices, local(): from_above = lax.ppermute(keep3, 'zh', down)  6.24 us
    ppermute x1, starting transfers between devices, local(): from_below = lax.ppermute(keep1, 'zh', up)  4.16 us
    ppermute x1, starting transfers between devices, local(): from_below = lax.ppermute(keep2[:104], 'zh', up)  3.66 us
    ppermute x1, waiting for transfers between devices, local(): from_below = lax.ppermute(keep2[:104], 'zh', up)  2.12 us
    ppermute x1, waiting for transfers between devices, local(): from_below = lax.ppermute(keep1, 'zh', up)  2.01 us
  transfers between devices with their start and end apart: 6, of which 5 were waited for; matrix products, arithmetic and copies ran while one was open for 0% of the time, Pallas kernels for 0%

profile of v4, /device:TPU:64, one launch (start us, length us, event | category | flops | bytes accessed | tf_op | source)
XLA Modules:
  0.0 75.3 jit_solution(14485801016685300632)
XLA Ops:
  0.7 0.1 copy-done
  0.7 0.1 fusion.5
  0.8 0.1 add_compare_fusion
  0.9 1.1 %bitcast_select_fusion = f32[144,648]{1,0:T(8,128)S(1)} fusion(f32[1,2,72,648]{3,2,1,0:T(8,128)} %param.14, pred[72,648]{1,0:T(8,128)(4,1)S(1)} %add_compare_fusion), kind=kLoop, calls=%fused_computation | loop fusion | flops 93312 | bytes 793152 | tf_op jit(solution)/shard_map/jit(_where)/select_n | solution.py:300
  2.0 0.0 copy-start.2
  2.1 0.9 %copy-done.2 = bf16[320,432]{1,0:T(8,128)(2,1)S(1)} copy-done((bf16[320,432]{1,0:T(8,128)(2,1)S(1)}, bf16[320,432]{1,0:T(8,128)(2,1)}, u32[]{:S(2)}) %copy-start.2) | copy-done | bytes 276504
  3.0 0.6 lines.1
  3.5 0.0 copy-start.1
  3.6 0.0 copy-start.3
  3.6 0.0 copy-start.4
  3.6 0.0 copy-start.5
  3.6 25.1 %all_to_all.10.r_ref = f32[32,56,128]{2,1,0:T(8,128)S(1)} all-to-all(f32[32,56,128]{2,1,0:T(8,128)S(1)} %lines.1), channel_id=1, replica_groups=mesh['yh'=2,'zh'=4,'zl'=2,'core'=2,'x'=4,'yl'=2] {'yh','x','yl','zl'}, dimensions={0} | all-to-all | bytes 1835008 | tf_op jit(solution)/shard_map/all_to_all | solution.py:310
  28.7 10.9 %planes.1 = (f32[216,128]{1,0:T(8,128)S(1)}, f32[216,128]{1,0:T(8,128)S(1)}, f32[216,128]{1,0:T(8,128)S(1)}, f32[216,128]{1,0:T(8,128)S(1)}, f32[216,128]{1,0:T(8,128)S(1)}, /*index=5*/f32[3,216,128]{2,1,0:T(8,128)S(1)}) custom-call(s32[5184]{0:T(1024)S(1)} %copy-done, f32[32,56,128]{2,1,0:T(8,128)S(1)} %all_to_all.10.r_ref, bf16[256,384]{1,0:T(8,128)(2,1)S(1)} %copy-done.5, ...), custom_call_target="tpu_custom_call" | custom-call | flops 10000000000 | bytes 2000000 | tf_op jit(solution)/shard_map/planes/pallas_call | solution.py:312
  39.6 0.1 collective-permute-start
  39.7 0.5 collective-permute-start.1
  40.2 1.3 %collective-permute-done.1 = f32[216,128]{1,0:T(8,128)S(1)} collective-permute-done((f32[216,128]{1,0:T(8,128)S(1)}, f32[216,128]{1,0:T(8,128)S(1)}, u32[]{:S(2)}, u32[]{:S(2)}) %collective-permute-start.1) | collective-permute-done | bytes 110624 | tf_op jit(solution)/shard_map/ppermute | solution.py:332
  41.5 3.7 %collective-permute-start.2 = (f32[104,128]{1,0:T(8,128)S(1)}, f32[104,128]{1,0:T(8,128)S(1)}, u32[]{:S(2)}, u32[]{:S(2)}) collective-permute-start(f32[104,128]{1,0:T(8,128)S(1)} %slice.39), channel_id=1, source_target_pairs={{0,32},{32,64},{64,96},{96,0},{1,33},{33,65},{65,97},{97,1},{2,34}... | collective-permute-start | bytes 159752 | tf_op jit(solution)/shard_map/ppermute | solution.py:334
  45.2 0.1 fusion
  45.3 2.1 %collective-permute-done.2 = f32[104,128]{1,0:T(8,128)S(1)} collective-permute-done((f32[104,128]{1,0:T(8,128)S(1)}, f32[104,128]{1,0:T(8,128)S(1)}, u32[]{:S(2)}, u32[]{:S(2)}) %collective-permute-start.2) | collective-permute-done | bytes 53280 | tf_op jit(solution)/shard_map/ppermute | solution.py:334
  47.4 0.0 copy-start.10
  47.4 0.0 copy-start.11
  47.5 4.2 %collective-permute-start.3 = (f32[216,128]{1,0:T(8,128)S(1)}, f32[216,128]{1,0:T(8,128)S(1)}, u32[]{:S(2)}, u32[]{:S(2)}) collective-permute-start(f32[216,128]{1,0:T(8,128)S(1)} %pad_maximum_fusion), channel_id=1, source_target_pairs={{0,32},{32,64},{64,96},{96,0},{1,33},{33,65},{65,97},{97,1},{2,34}... | collective-permute-start | bytes 331784 | tf_op jit(solution)/shard_map/ppermute | solution.py:340
  51.6 0.6 collective-permute-done.4
  52.2 0.0 copy-start.9
  52.3 0.1 collective-permute-start.5
  52.4 2.0 %collective-permute-done.3.r1_ref = f32[216,128]{1,0:T(8,128)S(1)} collective-permute-done((f32[216,128]{1,0:T(8,128)S(1)}, f32[216,128]{1,0:T(8,128)S(1)}, u32[]{:S(2)}, u32[]{:S(2)}) %collective-permute-start.3) | collective-permute-done | bytes 110624 | tf_op jit(solution)/shard_map/ppermute | solution.py:340
  54.4 6.2 %collective-permute-done.5.r2_ref = f32[216,128]{1,0:T(8,128)S(1)} collective-permute-done((f32[216,128]{1,0:T(8,128)S(1)}, f32[216,128]{1,0:T(8,128)S(1)}, u32[]{:S(2)}, u32[]{:S(2)}) %collective-permute-start.5) | collective-permute-done | bytes 110624 | tf_op jit(solution)/shard_map/ppermute | solution.py:341
  60.6 0.7 second.1
  61.3 0.0 copy-start.6
  61.3 0.0 copy-start.7
  61.3 12.6 %all_to_all.11.r_ref = f32[32,16,128]{2,1,0:T(8,128)S(1)} all-to-all(f32[32,16,128]{2,1,0:T(8,128)S(1)} %second.1), channel_id=1, replica_groups=mesh['yh'=2,'zh'=4,'zl'=2,'core'=2,'x'=4,'yl'=2] {'yh','x','yl','zl'}, dimensions={0} | all-to-all | bytes 524288 | tf_op jit(solution)/shard_map/all_to_all | solution.py:350
  73.9 1.4 %third.1 = f32[9,36,288]{2,1,0:T(8,128)} custom-call(f32[32,16,128]{2,1,0:T(8,128)S(1)} %all_to_all.11.r_ref, bf16[160,288]{1,0:T(8,128)(2,1)S(1)} %copy-done.7, bf16[160,288]{1,0:T(8,128)(2,1)S(1)} %copy-done.6), custom_call_target="tpu_custom_call" | custom-call | flops 1000000000 | bytes 2000000 | tf_op jit(solution)/shard_map/third/pallas_call | solution.py:351
  (25 shorter events, 0.1 us)
Async XLA Ops:
  0.0 0.7 copy-start
  2.0 1.0 %copy-start.2 = (bf16[320,432]{1,0:T(8,128)(2,1)S(1)}, bf16[320,432]{1,0:T(8,128)(2,1)}, u32[]{:S(2)}) copy-start(bf16[320,432]{1,0:T(8,128)(2,1)} %constant.68.clone.w_ref) | copy-start | bytes 829444
  3.5 25.1 %copy-start.1 = (bf16[2,160,432]{2,1,0:T(8,128)(2,1)S(1)}, bf16[2,160,432]{2,1,0:T(8,128)(2,1)}, u32[]{:S(2)}) copy-start(bf16[2,160,432]{2,1,0:T(8,128)(2,1)} %constant.72.clone.ug_ref) | copy-start | bytes 829444
  3.6 25.1 %copy-start.3 = (bf16[288,432]{1,0:T(8,128)(2,1)S(1)}, bf16[288,432]{1,0:T(8,128)(2,1)}, u32[]{:S(2)}) copy-start(bf16[288,432]{1,0:T(8,128)(2,1)} %constant.71.clone.er_ref) | copy-start | bytes 746500
  3.6 25.1 %copy-start.4 = (bf16[256,384]{1,0:T(8,128)(2,1)S(1)}, bf16[256,384]{1,0:T(8,128)(2,1)}, u32[]{:S(2)}) copy-start(bf16[256,384]{1,0:T(8,128)(2,1)} %constant.70.clone.elo_ref) | copy-start | bytes 589828
  3.6 25.1 %copy-start.5 = (bf16[256,384]{1,0:T(8,128)(2,1)S(1)}, bf16[256,384]{1,0:T(8,128)(2,1)}, u32[]{:S(2)}) copy-start(bf16[256,384]{1,0:T(8,128)(2,1)} %constant.69.clone.ehi_ref) | copy-start | bytes 589828
  39.6 5.6 %collective-permute-start = (f32[3,216,128]{2,1,0:T(8,128)S(1)}, f32[3,216,128]{2,1,0:T(8,128)S(1)}, u32[]{:S(2)}, u32[]{:S(2)}) collective-permute-start(f32[3,216,128]{2,1,0:T(8,128)S(1)} %get-tuple-element.12), channel_id=1, source_target_pairs={{0,8},{8,0},{1,9},{9,1},{2,10},{10,2},{3,11},{11,3},{4,12},{12,4},... | collective-permute-start | bytes 995336 | tf_op jit(solution)/shard_map/ppermute | solution.py:333
  39.7 1.8 %collective-permute-start.1 = (f32[216,128]{1,0:T(8,128)S(1)}, f32[216,128]{1,0:T(8,128)S(1)}, u32[]{:S(2)}, u32[]{:S(2)}) collective-permute-start(f32[216,128]{1,0:T(8,128)S(1)} %get-tuple-element.15), channel_id=1, source_target_pairs={{0,8},{8,0},{1,9},{9,1},{2,10},{10,2},{3,11},{11,3},{4,12},{12,4},... | collective-permute-start | bytes 331784 | tf_op jit(solution)/shard_map/ppermute | solution.py:332
  41.5 5.9 %collective-permute-start.2 = (f32[104,128]{1,0:T(8,128)S(1)}, f32[104,128]{1,0:T(8,128)S(1)}, u32[]{:S(2)}, u32[]{:S(2)}) collective-permute-start(f32[104,128]{1,0:T(8,128)S(1)} %slice.39), channel_id=1, source_target_pairs={{0,32},{32,64},{64,96},{96,0},{1,33},{33,65},{65,97},{97,1},{2,34}... | collective-permute-start | bytes 159752 | tf_op jit(solution)/shard_map/ppermute | solution.py:334
  45.2 7.0 %collective-permute-start.4 = (f32[112,128]{1,0:T(8,128)S(1)}, f32[112,128]{1,0:T(8,128)S(1)}, u32[]{:S(2)}, u32[]{:S(2)}) collective-permute-start(f32[112,128]{1,0:T(8,128)S(1)} %slice.44), channel_id=1, source_target_pairs={{0,96},{32,0},{64,32},{96,64},{1,97},{33,1},{65,33},{97,65},{2,98}... | collective-permute-start | bytes 172040 | tf_op jit(solution)/shard_map/ppermute | solution.py:335
  47.4 13.2 %copy-start.10 = (bf16[128,384]{1,0:T(8,128)(2,1)S(1)}, bf16[128,384]{1,0:T(8,128)(2,1)}, u32[]{:S(2)}) copy-start(bf16[128,384]{1,0:T(8,128)(2,1)} %constant.74.clone.flo_ref) | copy-start | bytes 294916
  47.4 13.2 %copy-start.11 = (bf16[128,384]{1,0:T(8,128)(2,1)S(1)}, bf16[128,384]{1,0:T(8,128)(2,1)}, u32[]{:S(2)}) copy-start(bf16[128,384]{1,0:T(8,128)(2,1)} %constant.73.clone.fhi_ref) | copy-start | bytes 294916
  47.5 6.9 %collective-permute-start.3 = (f32[216,128]{1,0:T(8,128)S(1)}, f32[216,128]{1,0:T(8,128)S(1)}, u32[]{:S(2)}, u32[]{:S(2)}) collective-permute-start(f32[216,128]{1,0:T(8,128)S(1)} %pad_maximum_fusion), channel_id=1, source_target_pairs={{0,32},{32,64},{64,96},{96,0},{1,33},{33,65},{65,97},{97,1},{2,34}... | collective-permute-start | bytes 331784 | tf_op jit(solution)/shard_map/ppermute | solution.py:340
  52.2 8.4 %copy-start.8 = (bf16[128,384]{1,0:T(8,128)(2,1)S(1)}, bf16[128,384]{1,0:T(8,128)(2,1)}, u32[]{:S(2)}) copy-start(bf16[128,384]{1,0:T(8,128)(2,1)} %constant.76.clone.tlo_ref) | copy-start | bytes 294916
  52.2 8.4 %copy-start.9 = (bf16[128,384]{1,0:T(8,128)(2,1)S(1)}, bf16[128,384]{1,0:T(8,128)(2,1)}, u32[]{:S(2)}) copy-start(bf16[128,384]{1,0:T(8,128)(2,1)} %constant.75.clone.thi_ref) | copy-start | bytes 294916
  52.3 8.3 %collective-permute-start.5 = (f32[216,128]{1,0:T(8,128)S(1)}, f32[216,128]{1,0:T(8,128)S(1)}, u32[]{:S(2)}, u32[]{:S(2)}) collective-permute-start(f32[216,128]{1,0:T(8,128)S(1)} %pad_maximum_fusion.1), channel_id=1, source_target_pairs={{0,96},{32,0},{64,32},{96,64},{1,97},{33,1},{65,33},{97,65},{2,98}... | collective-permute-start | bytes 331784 | tf_op jit(solution)/shard_map/ppermute | solution.py:341
  61.3 12.6 %copy-start.6 = (bf16[160,288]{1,0:T(8,128)(2,1)S(1)}, bf16[160,288]{1,0:T(8,128)(2,1)}, u32[]{:S(2)}) copy-start(bf16[160,288]{1,0:T(8,128)(2,1)} %constant.78.clone.ulo_ref) | copy-start | bytes 276484
  61.3 12.6 %copy-start.7 = (bf16[160,288]{1,0:T(8,128)(2,1)S(1)}, bf16[160,288]{1,0:T(8,128)(2,1)}, u32[]{:S(2)}) copy-start(bf16[160,288]{1,0:T(8,128)(2,1)} %constant.77.clone.uhi_ref) | copy-start | bytes 276484

commit v5 on v4

--- a/solution.py
+++ b/solution.py
@@ -149,13 +149,15 @@
         unpack(fb, 0)
     columns.wait()
 
+    views = [col_ref.at[pl.ds(t, NCOLS - 432 + 1)] for t in range(432)]
+
     def place(i, carry):
-        for t in range(216):
-            c = i * 216 + t
-            box[pl.ds(col_ref[c], 1), :] = st[pl.ds(c, 1), :]
+        at = i * 432
+        for t in range(432):
+            box[pl.ds(views[t][at], 1), :] = st[pl.ds(at + t, 1), :]
         return carry
 
-    lax.fori_loop(0, NCOLS // 216, place, 0)
+    lax.fori_loop(0, NCOLS // 432, place, 0)
 
     def along_second(i, carry):
         parts = []

time: 75.6 us -> 74.6 us (0.987)
  Pallas kernels: 13.5 us -> 12.6 us
    pallas_call x1, Pallas kernels: 10.9 us -> 9.99 us  [local(): call(k2_body, 'planes', [pl.BlockSpec(memory_space=pl.ANY)] + vmem(5), (b...]
where the time goes in v5:
time: 74.6 us; the launch traced here: 74.3 us
  blocking collectives  37.6 us (50%)
  Pallas kernels  12.6 us (17%)
  waiting for transfers between devices  12.2 us (16%)
  starting transfers between devices  8.48 us (11%)
  other arithmetic  1.37 us (2%)
  local copies, waits for them, and re-layouts  1.12 us (2%)
  between operations  0.89 us (1%)
    all_to_all x2, blocking collectives, local(): got = lax.all_to_all(sent, PLANE, split_axis=0, concat_axis=0, tiled=True)  37.6 us
    pallas_call x1, Pallas kernels, local(): call(k2_body, 'planes', [pl.BlockSpec(memory_space=pl.ANY)] + vmem(5), (b...  9.99 us
    ppermute x1, waiting for transfers between devices, local(): from_above = lax.ppermute(keep3, 'zh', down)  6.22 us
    ppermute x1, starting transfers between devices, local(): from_below = lax.ppermute(keep1, 'zh', up)  4.15 us
    ppermute x1, starting transfers between devices, local(): from_below = lax.ppermute(keep2[:104], 'zh', up)  3.66 us
    ppermute x1, waiting for transfers between devices, local(): from_below = lax.ppermute(keep2[:104], 'zh', up)  2.13 us
    ppermute x1, waiting for transfers between devices, local(): from_below = lax.ppermute(keep1, 'zh', up)  2.01 us
  transfers between devices with their start and end apart: 6, of which 5 were waited for; matrix products, arithmetic and copies ran while one was open for 0% of the time, Pallas kernels for 0%

profile of v5, /device:TPU:64, one launch (start us, length us, event | category | flops | bytes accessed | tf_op | source)
XLA Modules:
  0.0 74.3 jit_solution(15691794656246766268)
XLA Ops:
  0.7 0.1 copy-done
  0.7 0.1 fusion.5
  0.8 0.1 add_compare_fusion
  0.9 1.1 %bitcast_select_fusion = f32[144,648]{1,0:T(8,128)S(1)} fusion(f32[1,2,72,648]{3,2,1,0:T(8,128)} %param.14, pred[72,648]{1,0:T(8,128)(4,1)S(1)} %add_compare_fusion), kind=kLoop, calls=%fused_computation | loop fusion | flops 93312 | bytes 793152 | tf_op jit(solution)/shard_map/jit(_where)/select_n | solution.py:302
  2.0 0.0 copy-start.2
  2.1 0.9 %copy-done.2 = bf16[320,432]{1,0:T(8,128)(2,1)S(1)} copy-done((bf16[320,432]{1,0:T(8,128)(2,1)S(1)}, bf16[320,432]{1,0:T(8,128)(2,1)}, u32[]{:S(2)}) %copy-start.2) | copy-done | bytes 276504
  3.0 0.6 lines.1
  3.5 0.0 copy-start.1
  3.6 0.0 copy-start.4
  3.6 0.0 copy-start.5
  3.6 25.1 %all_to_all.10.r_ref = f32[32,56,128]{2,1,0:T(8,128)S(1)} all-to-all(f32[32,56,128]{2,1,0:T(8,128)S(1)} %lines.1), channel_id=1, replica_groups=mesh['yh'=2,'zh'=4,'zl'=2,'core'=2,'x'=4,'yl'=2] {'yh','x','yl','zl'}, dimensions={0} | all-to-all | bytes 1835008 | tf_op jit(solution)/shard_map/all_to_all | solution.py:312
  28.7 10.0 %planes.1 = (f32[216,128]{1,0:T(8,128)S(1)}, f32[216,128]{1,0:T(8,128)S(1)}, f32[216,128]{1,0:T(8,128)S(1)}, f32[216,128]{1,0:T(8,128)S(1)}, f32[216,128]{1,0:T(8,128)S(1)}, /*index=5*/f32[3,216,128]{2,1,0:T(8,128)S(1)}) custom-call(s32[5184]{0:T(1024)S(1)} %copy-done, f32[32,56,128]{2,1,0:T(8,128)S(1)} %all_to_all.10.r_ref, bf16[256,384]{1,0:T(8,128)(2,1)S(1)} %copy-done.5, ...), custom_call_target="tpu_custom_call" | custom-call | flops 10000000000 | bytes 2000000 | tf_op jit(solution)/shard_map/planes/pallas_call | solution.py:314
  38.7 0.1 collective-permute-start
  38.8 0.5 collective-permute-start.1
  39.3 1.3 %collective-permute-done.1 = f32[216,128]{1,0:T(8,128)S(1)} collective-permute-done((f32[216,128]{1,0:T(8,128)S(1)}, f32[216,128]{1,0:T(8,128)S(1)}, u32[]{:S(2)}, u32[]{:S(2)}) %collective-permute-start.1) | collective-permute-done | bytes 110624 | tf_op jit(solution)/shard_map/ppermute | solution.py:334
  40.6 3.7 %collective-permute-start.2 = (f32[104,128]{1,0:T(8,128)S(1)}, f32[104,128]{1,0:T(8,128)S(1)}, u32[]{:S(2)}, u32[]{:S(2)}) collective-permute-start(f32[104,128]{1,0:T(8,128)S(1)} %slice.39), channel_id=1, source_target_pairs={{0,32},{32,64},{64,96},{96,0},{1,33},{33,65},{65,97},{97,1},{2,34}... | collective-permute-start | bytes 159752 | tf_op jit(solution)/shard_map/ppermute | solution.py:336
  44.3 0.1 fusion
  44.4 2.1 %collective-permute-done.2 = f32[104,128]{1,0:T(8,128)S(1)} collective-permute-done((f32[104,128]{1,0:T(8,128)S(1)}, f32[104,128]{1,0:T(8,128)S(1)}, u32[]{:S(2)}, u32[]{:S(2)}) %collective-permute-start.2) | collective-permute-done | bytes 53280 | tf_op jit(solution)/shard_map/ppermute | solution.py:336
  46.5 0.0 copy-start.10
  46.5 0.0 copy-start.11
  46.5 4.1 %collective-permute-start.3 = (f32[216,128]{1,0:T(8,128)S(1)}, f32[216,128]{1,0:T(8,128)S(1)}, u32[]{:S(2)}, u32[]{:S(2)}) collective-permute-start(f32[216,128]{1,0:T(8,128)S(1)} %pad_maximum_fusion), channel_id=1, source_target_pairs={{0,32},{32,64},{64,96},{96,0},{1,33},{33,65},{65,97},{97,1},{2,34}... | collective-permute-start | bytes 331784 | tf_op jit(solution)/shard_map/ppermute | solution.py:342
  50.7 0.6 collective-permute-done.4
  51.3 0.0 copy-start.8
  51.3 0.0 copy-start.9
  51.3 0.1 collective-permute-start.5
  51.4 2.0 %collective-permute-done.3.r1_ref = f32[216,128]{1,0:T(8,128)S(1)} collective-permute-done((f32[216,128]{1,0:T(8,128)S(1)}, f32[216,128]{1,0:T(8,128)S(1)}, u32[]{:S(2)}, u32[]{:S(2)}) %collective-permute-start.3) | collective-permute-done | bytes 110624 | tf_op jit(solution)/shard_map/ppermute | solution.py:342
  53.5 6.2 %collective-permute-done.5.r2_ref = f32[216,128]{1,0:T(8,128)S(1)} collective-permute-done((f32[216,128]{1,0:T(8,128)S(1)}, f32[216,128]{1,0:T(8,128)S(1)}, u32[]{:S(2)}, u32[]{:S(2)}) %collective-permute-start.5) | collective-permute-done | bytes 110624 | tf_op jit(solution)/shard_map/ppermute | solution.py:343
  59.7 0.7 second.1
  60.4 0.0 copy-start.6
  60.4 0.0 copy-start.7
  60.4 12.6 %all_to_all.11.r_ref = f32[32,16,128]{2,1,0:T(8,128)S(1)} all-to-all(f32[32,16,128]{2,1,0:T(8,128)S(1)} %second.1), channel_id=1, replica_groups=mesh['yh'=2,'zh'=4,'zl'=2,'core'=2,'x'=4,'yl'=2] {'yh','x','yl','zl'}, dimensions={0} | all-to-all | bytes 524288 | tf_op jit(solution)/shard_map/all_to_all | solution.py:352
  73.0 1.4 %third.1 = f32[9,36,288]{2,1,0:T(8,128)} custom-call(f32[32,16,128]{2,1,0:T(8,128)S(1)} %all_to_all.11.r_ref, bf16[160,288]{1,0:T(8,128)(2,1)S(1)} %copy-done.7, bf16[160,288]{1,0:T(8,128)(2,1)S(1)} %copy-done.6), custom_call_target="tpu_custom_call" | custom-call | flops 1000000000 | bytes 2000000 | tf_op jit(solution)/shard_map/third/pallas_call | solution.py:353
  (25 shorter events, 0.1 us)
Async XLA Ops:
  0.0 0.7 copy-start
  2.0 1.0 %copy-start.2 = (bf16[320,432]{1,0:T(8,128)(2,1)S(1)}, bf16[320,432]{1,0:T(8,128)(2,1)}, u32[]{:S(2)}) copy-start(bf16[320,432]{1,0:T(8,128)(2,1)} %constant.68.clone.w_ref) | copy-start | bytes 829444
  3.5 25.1 %copy-start.1 = (bf16[2,160,432]{2,1,0:T(8,128)(2,1)S(1)}, bf16[2,160,432]{2,1,0:T(8,128)(2,1)}, u32[]{:S(2)}) copy-start(bf16[2,160,432]{2,1,0:T(8,128)(2,1)} %constant.72.clone.ug_ref) | copy-start | bytes 829444
  3.6 25.1 %copy-start.3 = (bf16[288,432]{1,0:T(8,128)(2,1)S(1)}, bf16[288,432]{1,0:T(8,128)(2,1)}, u32[]{:S(2)}) copy-start(bf16[288,432]{1,0:T(8,128)(2,1)} %constant.71.clone.er_ref) | copy-start | bytes 746500
  3.6 25.1 %copy-start.4 = (bf16[256,384]{1,0:T(8,128)(2,1)S(1)}, bf16[256,384]{1,0:T(8,128)(2,1)}, u32[]{:S(2)}) copy-start(bf16[256,384]{1,0:T(8,128)(2,1)} %constant.70.clone.elo_ref) | copy-start | bytes 589828
  3.6 25.1 %copy-start.5 = (bf16[256,384]{1,0:T(8,128)(2,1)S(1)}, bf16[256,384]{1,0:T(8,128)(2,1)}, u32[]{:S(2)}) copy-start(bf16[256,384]{1,0:T(8,128)(2,1)} %constant.69.clone.ehi_ref) | copy-start | bytes 589828
  38.7 5.6 %collective-permute-start = (f32[3,216,128]{2,1,0:T(8,128)S(1)}, f32[3,216,128]{2,1,0:T(8,128)S(1)}, u32[]{:S(2)}, u32[]{:S(2)}) collective-permute-start(f32[3,216,128]{2,1,0:T(8,128)S(1)} %get-tuple-element.12), channel_id=1, source_target_pairs={{0,8},{8,0},{1,9},{9,1},{2,10},{10,2},{3,11},{11,3},{4,12},{12,4},... | collective-permute-start | bytes 995336 | tf_op jit(solution)/shard_map/ppermute | solution.py:335
  38.8 1.8 %collective-permute-start.1 = (f32[216,128]{1,0:T(8,128)S(1)}, f32[216,128]{1,0:T(8,128)S(1)}, u32[]{:S(2)}, u32[]{:S(2)}) collective-permute-start(f32[216,128]{1,0:T(8,128)S(1)} %get-tuple-element.15), channel_id=1, source_target_pairs={{0,8},{8,0},{1,9},{9,1},{2,10},{10,2},{3,11},{11,3},{4,12},{12,4},... | collective-permute-start | bytes 331784 | tf_op jit(solution)/shard_map/ppermute | solution.py:334
  40.6 5.9 %collective-permute-start.2 = (f32[104,128]{1,0:T(8,128)S(1)}, f32[104,128]{1,0:T(8,128)S(1)}, u32[]{:S(2)}, u32[]{:S(2)}) collective-permute-start(f32[104,128]{1,0:T(8,128)S(1)} %slice.39), channel_id=1, source_target_pairs={{0,32},{32,64},{64,96},{96,0},{1,33},{33,65},{65,97},{97,1},{2,34}... | collective-permute-start | bytes 159752 | tf_op jit(solution)/shard_map/ppermute | solution.py:336
  44.3 7.0 %collective-permute-start.4 = (f32[112,128]{1,0:T(8,128)S(1)}, f32[112,128]{1,0:T(8,128)S(1)}, u32[]{:S(2)}, u32[]{:S(2)}) collective-permute-start(f32[112,128]{1,0:T(8,128)S(1)} %slice.44), channel_id=1, source_target_pairs={{0,96},{32,0},{64,32},{96,64},{1,97},{33,1},{65,33},{97,65},{2,98}... | collective-permute-start | bytes 172040 | tf_op jit(solution)/shard_map/ppermute | solution.py:337
  46.5 13.2 %copy-start.10 = (bf16[128,384]{1,0:T(8,128)(2,1)S(1)}, bf16[128,384]{1,0:T(8,128)(2,1)}, u32[]{:S(2)}) copy-start(bf16[128,384]{1,0:T(8,128)(2,1)} %constant.74.clone.flo_ref) | copy-start | bytes 294916
  46.5 13.2 %copy-start.11 = (bf16[128,384]{1,0:T(8,128)(2,1)S(1)}, bf16[128,384]{1,0:T(8,128)(2,1)}, u32[]{:S(2)}) copy-start(bf16[128,384]{1,0:T(8,128)(2,1)} %constant.73.clone.fhi_ref) | copy-start | bytes 294916
  46.5 6.9 %collective-permute-start.3 = (f32[216,128]{1,0:T(8,128)S(1)}, f32[216,128]{1,0:T(8,128)S(1)}, u32[]{:S(2)}, u32[]{:S(2)}) collective-permute-start(f32[216,128]{1,0:T(8,128)S(1)} %pad_maximum_fusion), channel_id=1, source_target_pairs={{0,32},{32,64},{64,96},{96,0},{1,33},{33,65},{65,97},{97,1},{2,34}... | collective-permute-start | bytes 331784 | tf_op jit(solution)/shard_map/ppermute | solution.py:342
  51.3 8.4 %copy-start.8 = (bf16[128,384]{1,0:T(8,128)(2,1)S(1)}, bf16[128,384]{1,0:T(8,128)(2,1)}, u32[]{:S(2)}) copy-start(bf16[128,384]{1,0:T(8,128)(2,1)} %constant.76.clone.tlo_ref) | copy-start | bytes 294916
  51.3 8.4 %copy-start.9 = (bf16[128,384]{1,0:T(8,128)(2,1)S(1)}, bf16[128,384]{1,0:T(8,128)(2,1)}, u32[]{:S(2)}) copy-start(bf16[128,384]{1,0:T(8,128)(2,1)} %constant.75.clone.thi_ref) | copy-start | bytes 294916
  51.3 8.3 %collective-permute-start.5 = (f32[216,128]{1,0:T(8,128)S(1)}, f32[216,128]{1,0:T(8,128)S(1)}, u32[]{:S(2)}, u32[]{:S(2)}) collective-permute-start(f32[216,128]{1,0:T(8,128)S(1)} %pad_maximum_fusion.1), channel_id=1, source_target_pairs={{0,96},{32,0},{64,32},{96,64},{1,97},{33,1},{65,33},{97,65},{2,98}... | collective-permute-start | bytes 331784 | tf_op jit(solution)/shard_map/ppermute | solution.py:343
  60.4 12.6 %copy-start.6 = (bf16[160,288]{1,0:T(8,128)(2,1)S(1)}, bf16[160,288]{1,0:T(8,128)(2,1)}, u32[]{:S(2)}) copy-start(bf16[160,288]{1,0:T(8,128)(2,1)} %constant.78.clone.ulo_ref) | copy-start | bytes 276484
  60.4 12.6 %copy-start.7 = (bf16[160,288]{1,0:T(8,128)(2,1)S(1)}, bf16[160,288]{1,0:T(8,128)(2,1)}, u32[]{:S(2)}) copy-start(bf16[160,288]{1,0:T(8,128)(2,1)} %constant.77.clone.uhi_ref) | copy-start | bytes 276484

commit v6 on v5

--- a/solution.py
+++ b/solution.py
@@ -17,7 +17,7 @@
 AXES = ("yh", "zh", "zl", "core", "x", "yl")
 SIZES = (2, 4, 2, 2, 4, 2)
 BAND, FFT = ("yh", "zh", "zl", "core"), ("x", "yl")
-PLANE = ("yh", "x", "yl", "zl")
+PLANE = ("zl", "yh", "yl", "x")
 ND = 32
 NB = 4
 NP = 5
@@ -118,12 +118,20 @@
         o_ref[q, 55:56, :] = weight
 
 
+def rank(yh, fb, zl):
+    at = {"yh": yh, "x": fb // 2, "yl": fb % 2, "zl": zl}
+    place = 0
+    for axis in PLANE:
+        place = place * SIZES[AXES.index(axis)] + at[axis]
+    return place
+
+
 def source(b, fb):
-    return 16 * (b // 2) + 2 * fb + b % 2
+    return rank(b // 2, fb, b % 2)
 
 
 def k2_body(row_ref, r_ref, ehi_ref, elo_ref, er_ref, ug_ref, *rest):
-    keep2, keep0, keep1, keep3, send2, send_rest, tr, st, box, hs, gs, col_ref, sem = rest
+    keep2, keep0, keep1, keep3, send, tr, st, box, hs, gs, col_ref, sem = rest
     columns = pltpu.make_async_copy(row_ref, col_ref, sem)
     columns.start()
     core = lax.axis_index("core")
@@ -210,7 +218,7 @@
     for p in range(NP):
         plane(p, 0)
     tail_lane = lanes((36, 128))
-    sends = [send_rest.at[0], send_rest.at[1], send2, send_rest.at[2]]
+    sends = [send.at[d] for d in range(4)]
     for part, outs in enumerate(((keep0, keep1, keep2, keep3), sends)):
         for d in range(4):
             z = (zh + d) & 3
@@ -250,7 +258,7 @@
                         if a != v:
                             part = pltpu.roll(part, (36 * (a - v)) % 128, 1)
                         acc = part if acc is None else jnp.where(lane < 36 * a, acc, part)
-                    o_ref[16 * yh + 2 * fb + zl, NP * b : NP * b + NP, :] = acc
+                    o_ref[rank(yh, fb, zl), NP * b : NP * b + NP, :] = acc
 
 
 def k4_body(r_ref, uhi_ref, ulo_ref, o_ref, xs, ys):
@@ -311,11 +319,11 @@
     )(occupation, masked, fold(w1, 1))
     got = lax.all_to_all(sent, PLANE, split_axis=0, concat_axis=0, tiled=True)
     block = shape(R2ROWS, 128)
-    keep2, keep0, keep1, keep3, send2, send_rest = call(
+    keep2, keep0, keep1, keep3, send = call(
         k2_body,
         "planes",
         [pl.BlockSpec(memory_space=pl.ANY)] + vmem(5),
-        (block, block, block, block, block, shape(3, R2ROWS, 128)),
+        (block, block, block, block, shape(4, R2ROWS, 128)),
         [
             (48, 48, 128),
             (NCOLS, 128),
@@ -331,12 +339,12 @@
     swap = [(0, 1), (1, 0)]
     up = [(i, (i + 1) % 4) for i in range(4)]
     down = [(i, (i - 1) % 4) for i in range(4)]
-    keep2 = keep2 + lax.ppermute(send2, "core", swap)
-    rest = lax.ppermute(send_rest, "core", swap)
+    swapped = lax.ppermute(send, "core", swap)
+    keep2 = keep2 + swapped[2]
     from_below = lax.ppermute(keep2[:104], "zh", up)
     from_above = lax.ppermute(keep2[104:], "zh", down)
-    keep1 = keep1 + rest[1]
-    keep3 = keep3 + rest[2]
+    keep1 = keep1 + swapped[1]
+    keep3 = keep3 + swapped[3]
     keep1 = jnp.concatenate([keep1[:104] + from_below, keep1[104:]], 0)
     keep3 = jnp.concatenate([keep3[:104], keep3[104:] + from_above], 0)
     from_below = lax.ppermute(keep1, "zh", up)
@@ -348,7 +356,7 @@
         shape(ND, R3ROWS, 128),
         [(R2ROWS, 128), (184, 128), (3, 184, 128)],
         10**9,
-    )(keep0 + rest[0], from_below, from_above, fhi, flo, thi, tlo)
+    )(keep0 + swapped[0], from_below, from_above, fhi, flo, thi, tlo)
     got = lax.all_to_all(sent, PLANE, split_axis=0, concat_axis=0, tiled=True)
     return call(
         k4_body, "third", vmem(3), shape(9, 36, NF), [(3, NZ, 128), (3, 128, NF)], 10**9

time: 74.6 us -> 74.7 us (level)
    ppermute x1, waiting for transfers between devices: 2.01 us -> 3.85 us  [local(): from_below = lax.ppermute(keep1, 'zh', up)]
    ppermute x1, waiting for transfers between devices: 6.22 us -> 4.5 us  [local(): from_above = lax.ppermute(keep3, 'zh', down)]
    ppermute x2 -> x1, waiting for transfers between devices: 1.29 us -> 1.78 us  [local(): swapped = lax.ppermute(send, 'core', swap)]
  transfers between devices with their start and end apart: 6 -> 5, of which waited for: 5 -> 5; matrix products, arithmetic and copies ran while one was open for 0% -> 0% of each run, Pallas kernels for 0% -> 0%
where the time goes in v6:
time: 74.7 us; the launch traced here: 74.4 us
  blocking collectives  37 us (50%)
  waiting for transfers between devices  12.8 us (17%)
  Pallas kernels  12.6 us (17%)
  starting transfers between devices  8.59 us (11%)
  other arithmetic  1.36 us (2%)
  local copies, waits for them, and re-layouts  1.11 us (1%)
  between operations  0.87 us (1%)
    all_to_all x2, blocking collectives, local(): got = lax.all_to_all(sent, PLANE, split_axis=0, concat_axis=0, tiled=True)  37 us
    pallas_call x1, Pallas kernels, local(): call(k2_body, 'planes', [pl.BlockSpec(memory_space=pl.ANY)] + vmem(5), (b...  10 us
    ppermute x1, starting transfers between devices, local(): from_below = lax.ppermute(keep1, 'zh', up)  4.67 us
    ppermute x1, waiting for transfers between devices, local(): from_above = lax.ppermute(keep3, 'zh', down)  4.5 us
    ppermute x1, waiting for transfers between devices, local(): from_below = lax.ppermute(keep1, 'zh', up)  3.85 us
    ppermute x1, starting transfers between devices, local(): from_below = lax.ppermute(keep2[:104], 'zh', up)  3.66 us
    ppermute x1, waiting for transfers between devices, local(): from_below = lax.ppermute(keep2[:104], 'zh', up)  2.05 us
    ppermute x1, waiting for transfers between devices, local(): swapped = lax.ppermute(send, 'core', swap)  1.78 us
  transfers between devices with their start and end apart: 5, of which 5 were waited for; matrix products, arithmetic and copies ran while one was open for 0% of the time, Pallas kernels for 0%

profile of v6, /device:TPU:64, one launch (start us, length us, event | category | flops | bytes accessed | tf_op | source)
XLA Modules:
  0.0 74.4 jit_solution(6165601508310662912)
XLA Ops:
  0.7 0.1 copy-done
  0.7 0.1 fusion.6
  0.8 0.1 add_compare_fusion
  0.9 1.1 %bitcast_select_fusion = f32[144,648]{1,0:T(8,128)S(1)} fusion(f32[1,2,72,648]{3,2,1,0:T(8,128)} %param.14, pred[72,648]{1,0:T(8,128)(4,1)S(1)} %add_compare_fusion), kind=kLoop, calls=%fused_computation | loop fusion | flops 93312 | bytes 793152 | tf_op jit(solution)/shard_map/jit(_where)/select_n | solution.py:310
  2.0 0.0 copy-start.2
  2.1 0.9 %copy-done.2 = bf16[320,432]{1,0:T(8,128)(2,1)S(1)} copy-done((bf16[320,432]{1,0:T(8,128)(2,1)S(1)}, bf16[320,432]{1,0:T(8,128)(2,1)}, u32[]{:S(2)}) %copy-start.2) | copy-done | bytes 276504
  3.0 0.6 lines.1
  3.5 0.0 copy-start.1
  3.6 0.0 copy-start.3
  3.6 0.0 copy-start.4
  3.6 0.0 copy-start.5
  3.6 23.9 %all_to_all.10.r_ref = f32[32,56,128]{2,1,0:T(8,128)S(1)} all-to-all(f32[32,56,128]{2,1,0:T(8,128)S(1)} %lines.1), channel_id=1, replica_groups=mesh['yh'=2,'zh'=4,'zl'=2,'core'=2,'x'=4,'yl'=2] {'zl','yh','yl','x'}, dimensions={0} | all-to-all | bytes 1835008 | tf_op jit(solution)/shard_map/all_to_all | solution.py:320
  27.5 0.0 copy-done.3
  27.5 10.0 %planes.1 = (f32[216,128]{1,0:T(8,128)S(1)}, f32[216,128]{1,0:T(8,128)S(1)}, f32[216,128]{1,0:T(8,128)S(1)}, f32[216,128]{1,0:T(8,128)S(1)}, f32[4,216,128]{2,1,0:T(8,128)S(1)}) custom-call(s32[5184]{0:T(1024)S(1)} %copy-done, f32[32,56,128]{2,1,0:T(8,128)S(1)} %all_to_all.10.r_ref, bf16[256,384]{1,0:T(8,128)(2,1)S(1)} %copy-done.5, ...), custom_call_target="tpu_custom_call" | custom-call | flops 10000000000 | bytes 2000000 | tf_op jit(solution)/shard_map/planes/pallas_call | solution.py:322
  37.5 0.1 collective-permute-start
  37.6 1.8 %collective-permute-done = f32[4,216,128]{2,1,0:T(8,128)S(1)} collective-permute-done((f32[4,216,128]{2,1,0:T(8,128)S(1)}, f32[4,216,128]{2,1,0:T(8,128)S(1)}, u32[]{:S(2)}, u32[]{:S(2)}) %collective-permute-start) | collective-permute-done | bytes 442400 | tf_op jit(solution)/shard_map/ppermute | solution.py:342
  39.4 0.1 fusion
  39.5 3.7 %collective-permute-start.1 = (f32[104,128]{1,0:T(8,128)S(1)}, f32[104,128]{1,0:T(8,128)S(1)}, u32[]{:S(2)}, u32[]{:S(2)}) collective-permute-start(f32[104,128]{1,0:T(8,128)S(1)} %slice.44), channel_id=1, source_target_pairs={{0,32},{32,64},{64,96},{96,0},{1,33},{33,65},{65,97},{97,1},{2,34}... | collective-permute-start | bytes 159752 | tf_op jit(solution)/shard_map/ppermute | solution.py:344
  43.2 0.1 collective-permute-start.3
  43.3 2.1 %collective-permute-done.1 = f32[104,128]{1,0:T(8,128)S(1)} collective-permute-done((f32[104,128]{1,0:T(8,128)S(1)}, f32[104,128]{1,0:T(8,128)S(1)}, u32[]{:S(2)}, u32[]{:S(2)}) %collective-permute-start.1) | collective-permute-done | bytes 53280 | tf_op jit(solution)/shard_map/ppermute | solution.py:344
  45.4 4.7 %collective-permute-start.2 = (f32[216,128]{1,0:T(8,128)S(1)}, f32[216,128]{1,0:T(8,128)S(1)}, u32[]{:S(2)}, u32[]{:S(2)}) collective-permute-start(f32[216,128]{1,0:T(8,128)S(1)} %pad_maximum_fusion), channel_id=1, source_target_pairs={{0,32},{32,64},{64,96},{96,0},{1,33},{33,65},{65,97},{97,1},{2,34}... | collective-permute-start | bytes 331784 | tf_op jit(solution)/shard_map/ppermute | solution.py:350
  50.0 0.6 collective-permute-done.3
  50.7 0.0 copy-start.8
  50.7 0.0 copy-start.9
  50.7 0.1 collective-permute-start.4
  50.8 3.8 %collective-permute-done.2.r1_ref = f32[216,128]{1,0:T(8,128)S(1)} collective-permute-done((f32[216,128]{1,0:T(8,128)S(1)}, f32[216,128]{1,0:T(8,128)S(1)}, u32[]{:S(2)}, u32[]{:S(2)}) %collective-permute-start.2) | collective-permute-done | bytes 110624 | tf_op jit(solution)/shard_map/ppermute | solution.py:350
  54.7 4.5 %collective-permute-done.4.r2_ref = f32[216,128]{1,0:T(8,128)S(1)} collective-permute-done((f32[216,128]{1,0:T(8,128)S(1)}, f32[216,128]{1,0:T(8,128)S(1)}, u32[]{:S(2)}, u32[]{:S(2)}) %collective-permute-start.4) | collective-permute-done | bytes 110624 | tf_op jit(solution)/shard_map/ppermute | solution.py:351
  59.2 0.7 second.1
  59.9 0.0 copy-start.6
  59.9 0.0 copy-start.7
  59.9 13.1 %all_to_all.11.r_ref = f32[32,16,128]{2,1,0:T(8,128)S(1)} all-to-all(f32[32,16,128]{2,1,0:T(8,128)S(1)} %second.1), channel_id=1, replica_groups=mesh['yh'=2,'zh'=4,'zl'=2,'core'=2,'x'=4,'yl'=2] {'zl','yh','yl','x'}, dimensions={0} | all-to-all | bytes 524288 | tf_op jit(solution)/shard_map/all_to_all | solution.py:360
  73.0 1.4 %third.1 = f32[9,36,288]{2,1,0:T(8,128)} custom-call(f32[32,16,128]{2,1,0:T(8,128)S(1)} %all_to_all.11.r_ref, bf16[160,288]{1,0:T(8,128)(2,1)S(1)} %copy-done.7, bf16[160,288]{1,0:T(8,128)(2,1)S(1)} %copy-done.6), custom_call_target="tpu_custom_call" | custom-call | flops 1000000000 | bytes 2000000 | tf_op jit(solution)/shard_map/third/pallas_call | solution.py:361
  (22 shorter events, 0.1 us)
Async XLA Ops:
  0.0 0.7 copy-start
  2.0 1.0 %copy-start.2 = (bf16[320,432]{1,0:T(8,128)(2,1)S(1)}, bf16[320,432]{1,0:T(8,128)(2,1)}, u32[]{:S(2)}) copy-start(bf16[320,432]{1,0:T(8,128)(2,1)} %constant.68.clone.w_ref) | copy-start | bytes 829444
  3.5 24.0 %copy-start.1 = (bf16[2,160,432]{2,1,0:T(8,128)(2,1)S(1)}, bf16[2,160,432]{2,1,0:T(8,128)(2,1)}, u32[]{:S(2)}) copy-start(bf16[2,160,432]{2,1,0:T(8,128)(2,1)} %constant.72.clone.ug_ref) | copy-start | bytes 829444
  3.6 24.0 %copy-start.3 = (bf16[288,432]{1,0:T(8,128)(2,1)S(1)}, bf16[288,432]{1,0:T(8,128)(2,1)}, u32[]{:S(2)}) copy-start(bf16[288,432]{1,0:T(8,128)(2,1)} %constant.71.clone.er_ref) | copy-start | bytes 746500
  3.6 23.9 %copy-start.4 = (bf16[256,384]{1,0:T(8,128)(2,1)S(1)}, bf16[256,384]{1,0:T(8,128)(2,1)}, u32[]{:S(2)}) copy-start(bf16[256,384]{1,0:T(8,128)(2,1)} %constant.70.clone.elo_ref) | copy-start | bytes 589828
  3.6 23.9 %copy-start.5 = (bf16[256,384]{1,0:T(8,128)(2,1)S(1)}, bf16[256,384]{1,0:T(8,128)(2,1)}, u32[]{:S(2)}) copy-start(bf16[256,384]{1,0:T(8,128)(2,1)} %constant.69.clone.ehi_ref) | copy-start | bytes 589828
  37.5 1.9 %collective-permute-start = (f32[4,216,128]{2,1,0:T(8,128)S(1)}, f32[4,216,128]{2,1,0:T(8,128)S(1)}, u32[]{:S(2)}, u32[]{:S(2)}) collective-permute-start(f32[4,216,128]{2,1,0:T(8,128)S(1)} %get-tuple-element.11), channel_id=1, source_target_pairs={{0,8},{8,0},{1,9},{9,1},{2,10},{10,2},{3,11},{11,3},{4,12},{12,4},... | collective-permute-start | bytes 1327112 | tf_op jit(solution)/shard_map/ppermute | solution.py:342
  39.5 5.8 %collective-permute-start.1 = (f32[104,128]{1,0:T(8,128)S(1)}, f32[104,128]{1,0:T(8,128)S(1)}, u32[]{:S(2)}, u32[]{:S(2)}) collective-permute-start(f32[104,128]{1,0:T(8,128)S(1)} %slice.44), channel_id=1, source_target_pairs={{0,32},{32,64},{64,96},{96,0},{1,33},{33,65},{65,97},{97,1},{2,34}... | collective-permute-start | bytes 159752 | tf_op jit(solution)/shard_map/ppermute | solution.py:344
  43.2 7.5 %collective-permute-start.3 = (f32[112,128]{1,0:T(8,128)S(1)}, f32[112,128]{1,0:T(8,128)S(1)}, u32[]{:S(2)}, u32[]{:S(2)}) collective-permute-start(f32[112,128]{1,0:T(8,128)S(1)} %slice.49), channel_id=1, source_target_pairs={{0,96},{32,0},{64,32},{96,64},{1,97},{33,1},{65,33},{97,65},{2,98}... | collective-permute-start | bytes 172040 | tf_op jit(solution)/shard_map/ppermute | solution.py:345
  45.3 13.8 %copy-start.10 = (bf16[128,384]{1,0:T(8,128)(2,1)S(1)}, bf16[128,384]{1,0:T(8,128)(2,1)}, u32[]{:S(2)}) copy-start(bf16[128,384]{1,0:T(8,128)(2,1)} %constant.74.clone.flo_ref) | copy-start | bytes 294916
  45.3 13.8 %copy-start.11 = (bf16[128,384]{1,0:T(8,128)(2,1)S(1)}, bf16[128,384]{1,0:T(8,128)(2,1)}, u32[]{:S(2)}) copy-start(bf16[128,384]{1,0:T(8,128)(2,1)} %constant.73.clone.fhi_ref) | copy-start | bytes 294916
  45.4 9.3 %collective-permute-start.2 = (f32[216,128]{1,0:T(8,128)S(1)}, f32[216,128]{1,0:T(8,128)S(1)}, u32[]{:S(2)}, u32[]{:S(2)}) collective-permute-start(f32[216,128]{1,0:T(8,128)S(1)} %pad_maximum_fusion), channel_id=1, source_target_pairs={{0,32},{32,64},{64,96},{96,0},{1,33},{33,65},{65,97},{97,1},{2,34}... | collective-permute-start | bytes 331784 | tf_op jit(solution)/shard_map/ppermute | solution.py:350
  50.7 8.5 %copy-start.8 = (bf16[128,384]{1,0:T(8,128)(2,1)S(1)}, bf16[128,384]{1,0:T(8,128)(2,1)}, u32[]{:S(2)}) copy-start(bf16[128,384]{1,0:T(8,128)(2,1)} %constant.76.clone.tlo_ref) | copy-start | bytes 294916
  50.7 8.5 %copy-start.9 = (bf16[128,384]{1,0:T(8,128)(2,1)S(1)}, bf16[128,384]{1,0:T(8,128)(2,1)}, u32[]{:S(2)}) copy-start(bf16[128,384]{1,0:T(8,128)(2,1)} %constant.75.clone.thi_ref) | copy-start | bytes 294916
  50.7 8.4 %collective-permute-start.4 = (f32[216,128]{1,0:T(8,128)S(1)}, f32[216,128]{1,0:T(8,128)S(1)}, u32[]{:S(2)}, u32[]{:S(2)}) collective-permute-start(f32[216,128]{1,0:T(8,128)S(1)} %pad_maximum_fusion.1), channel_id=1, source_target_pairs={{0,96},{32,0},{64,32},{96,64},{1,97},{33,1},{65,33},{97,65},{2,98}... | collective-permute-start | bytes 331784 | tf_op jit(solution)/shard_map/ppermute | solution.py:351
  59.9 13.2 %copy-start.6 = (bf16[160,288]{1,0:T(8,128)(2,1)S(1)}, bf16[160,288]{1,0:T(8,128)(2,1)}, u32[]{:S(2)}) copy-start(bf16[160,288]{1,0:T(8,128)(2,1)} %constant.78.clone.ulo_ref) | copy-start | bytes 276484
  59.9 13.1 %copy-start.7 = (bf16[160,288]{1,0:T(8,128)(2,1)S(1)}, bf16[160,288]{1,0:T(8,128)(2,1)}, u32[]{:S(2)}) copy-start(bf16[160,288]{1,0:T(8,128)(2,1)} %constant.77.clone.uhi_ref) | copy-start | bytes 276484

commit v7 on v6

--- a/solution.py
+++ b/solution.py
@@ -17,7 +17,7 @@
 AXES = ("yh", "zh", "zl", "core", "x", "yl")
 SIZES = (2, 4, 2, 2, 4, 2)
 BAND, FFT = ("yh", "zh", "zl", "core"), ("x", "yl")
-PLANE = ("zl", "yh", "yl", "x")
+PLANE = ("yh", "x", "yl", "zl")
 ND = 32
 NB = 4
 NP = 5
@@ -118,16 +118,8 @@
         o_ref[q, 55:56, :] = weight
 
 
-def rank(yh, fb, zl):
-    at = {"yh": yh, "x": fb // 2, "yl": fb % 2, "zl": zl}
-    place = 0
-    for axis in PLANE:
-        place = place * SIZES[AXES.index(axis)] + at[axis]
-    return place
-
-
 def source(b, fb):
-    return rank(b // 2, fb, b % 2)
+    return 16 * (b // 2) + 2 * fb + b % 2
 
 
 def k2_body(row_ref, r_ref, ehi_ref, elo_ref, er_ref, ug_ref, *rest):
@@ -169,17 +161,17 @@
 
     def along_second(i, carry):
         parts = []
-        for t in range(36):
-            at = pl.multiple_of((i * 36 + t) * KZ, 8)
+        for t in range(72):
+            at = (i * 72 + t) * KZ
             flipped = box[pl.ds(at, 128), :].T
             parts.append(jnp.concatenate([flipped[0:24], flipped[24:48]], 1))
         line = jnp.concatenate(parts, 0)
         half = dot3(line, ehi_ref[...], elo_ref[...])
         for j in range(3):
-            hs[j, pl.ds(pl.multiple_of(i * 864, 8), 864), :] = half[:, 128 * j : 128 * j + 128]
+            hs[j, pl.ds(i * 1728, 1728), :] = half[:, 128 * j : 128 * j + 128]
         return carry
 
-    lax.fori_loop(0, 2, along_second, 0)
+    along_second(0, 0)
 
     lane = lanes((NC, 128))
 
@@ -258,7 +250,7 @@
                         if a != v:
                             part = pltpu.roll(part, (36 * (a - v)) % 128, 1)
                         acc = part if acc is None else jnp.where(lane < 36 * a, acc, part)
-                    o_ref[rank(yh, fb, zl), NP * b : NP * b + NP, :] = acc
+                    o_ref[16 * yh + 2 * fb + zl, NP * b : NP * b + NP, :] = acc
 
 
 def k4_body(r_ref, uhi_ref, ulo_ref, o_ref, xs, ys):
@@ -334,7 +326,7 @@
             pltpu.SemaphoreType.DMA,
         ],
         10**10,
-        24,
+        32,
     )(col_index, got, ehi, elo, fold(er, 1), fold(ug, 2))
     swap = [(0, 1), (1, 0)]
     up = [(i, (i + 1) % 4) for i in range(4)]

time: 74.7 us -> 74.6 us (level)
    ppermute x1, waiting for transfers between devices: 4.5 us -> 6.33 us  [local(): from_above = lax.ppermute(keep3, 'zh', down)]
    ppermute x1, waiting for transfers between devices: 3.85 us -> 2.13 us  [local(): from_below = lax.ppermute(keep1, 'zh', up)]
where the time goes in v7:
time: 74.6 us; the launch traced here: 74.3 us
  blocking collectives  37.6 us (50%)
  waiting for transfers between devices  12.8 us (17%)
  Pallas kernels  12.4 us (17%)
  starting transfers between devices  8.09 us (11%)
  other arithmetic  1.36 us (2%)
  local copies, waits for them, and re-layouts  1.11 us (1%)
  between operations  0.87 us (1%)
    all_to_all x2, blocking collectives, local(): got = lax.all_to_all(sent, PLANE, split_axis=0, concat_axis=0, tiled=True)  37.6 us
    pallas_call x1, Pallas kernels, local(): call(k2_body, 'planes', [pl.BlockSpec(memory_space=pl.ANY)] + vmem(5), (b...  9.82 us
    ppermute x1, waiting for transfers between devices, local(): from_above = lax.ppermute(keep3, 'zh', down)  6.33 us
    ppermute x1, starting transfers between devices, local(): from_below = lax.ppermute(keep1, 'zh', up)  4.15 us
    ppermute x1, starting transfers between devices, local(): from_below = lax.ppermute(keep2[:104], 'zh', up)  3.68 us
    ppermute x1, waiting for transfers between devices, local(): from_below = lax.ppermute(keep1, 'zh', up)  2.13 us
    ppermute x1, waiting for transfers between devices, local(): from_below = lax.ppermute(keep2[:104], 'zh', up)  2.08 us
    ppermute x1, waiting for transfers between devices, local(): swapped = lax.ppermute(send, 'core', swap)  1.78 us
  transfers between devices with their start and end apart: 5, of which 5 were waited for; matrix products, arithmetic and copies ran while one was open for 0% of the time, Pallas kernels for 0%

profile of v7, /device:TPU:64, one launch (start us, length us, event | category | flops | bytes accessed | tf_op | source)
XLA Modules:
  0.0 74.3 jit_solution(3862521586126969518)
XLA Ops:
  0.7 0.1 copy-done
  0.7 0.1 fusion.6
  0.8 0.1 add_compare_fusion
  0.9 1.1 %bitcast_select_fusion = f32[144,648]{1,0:T(8,128)S(1)} fusion(f32[1,2,72,648]{3,2,1,0:T(8,128)} %param.14, pred[72,648]{1,0:T(8,128)(4,1)S(1)} %add_compare_fusion), kind=kLoop, calls=%fused_computation | loop fusion | flops 93312 | bytes 793152 | tf_op jit(solution)/shard_map/jit(_where)/select_n | solution.py:302
  2.0 0.0 copy-start.2
  2.1 0.9 %copy-done.2 = bf16[320,432]{1,0:T(8,128)(2,1)S(1)} copy-done((bf16[320,432]{1,0:T(8,128)(2,1)S(1)}, bf16[320,432]{1,0:T(8,128)(2,1)}, u32[]{:S(2)}) %copy-start.2) | copy-done | bytes 276504
  3.0 0.6 lines.1
  3.5 0.0 copy-start.1
  3.6 0.0 copy-start.3
  3.6 0.0 copy-start.4
  3.6 0.0 copy-start.5
  3.6 25.1 %all_to_all.10.r_ref = f32[32,56,128]{2,1,0:T(8,128)S(1)} all-to-all(f32[32,56,128]{2,1,0:T(8,128)S(1)} %lines.1), channel_id=1, replica_groups=mesh['yh'=2,'zh'=4,'zl'=2,'core'=2,'x'=4,'yl'=2] {'yh','x','yl','zl'}, dimensions={0} | all-to-all | bytes 1835008 | tf_op jit(solution)/shard_map/all_to_all | solution.py:312
  28.7 0.0 copy-done.3
  28.7 9.8 %planes.1 = (f32[216,128]{1,0:T(8,128)S(1)}, f32[216,128]{1,0:T(8,128)S(1)}, f32[216,128]{1,0:T(8,128)S(1)}, f32[216,128]{1,0:T(8,128)S(1)}, f32[4,216,128]{2,1,0:T(8,128)S(1)}) custom-call(s32[5184]{0:T(1024)S(1)} %copy-done, f32[32,56,128]{2,1,0:T(8,128)S(1)} %all_to_all.10.r_ref, bf16[256,384]{1,0:T(8,128)(2,1)S(1)} %copy-done.5, ...), custom_call_target="tpu_custom_call" | custom-call | flops 10000000000 | bytes 2000000 | tf_op jit(solution)/shard_map/planes/pallas_call | solution.py:314
  38.5 0.1 collective-permute-start
  38.6 1.8 %collective-permute-done = f32[4,216,128]{2,1,0:T(8,128)S(1)} collective-permute-done((f32[4,216,128]{2,1,0:T(8,128)S(1)}, f32[4,216,128]{2,1,0:T(8,128)S(1)}, u32[]{:S(2)}, u32[]{:S(2)}) %collective-permute-start) | collective-permute-done | bytes 442400 | tf_op jit(solution)/shard_map/ppermute | solution.py:334
  40.4 0.1 fusion
  40.5 3.7 %collective-permute-start.1 = (f32[104,128]{1,0:T(8,128)S(1)}, f32[104,128]{1,0:T(8,128)S(1)}, u32[]{:S(2)}, u32[]{:S(2)}) collective-permute-start(f32[104,128]{1,0:T(8,128)S(1)} %slice.44), channel_id=1, source_target_pairs={{0,32},{32,64},{64,96},{96,0},{1,33},{33,65},{65,97},{97,1},{2,34}... | collective-permute-start | bytes 159752 | tf_op jit(solution)/shard_map/ppermute | solution.py:336
  44.2 0.1 collective-permute-start.3
  44.3 2.1 %collective-permute-done.1 = f32[104,128]{1,0:T(8,128)S(1)} collective-permute-done((f32[104,128]{1,0:T(8,128)S(1)}, f32[104,128]{1,0:T(8,128)S(1)}, u32[]{:S(2)}, u32[]{:S(2)}) %collective-permute-start.1) | collective-permute-done | bytes 53280 | tf_op jit(solution)/shard_map/ppermute | solution.py:336
  46.4 4.2 %collective-permute-start.2 = (f32[216,128]{1,0:T(8,128)S(1)}, f32[216,128]{1,0:T(8,128)S(1)}, u32[]{:S(2)}, u32[]{:S(2)}) collective-permute-start(f32[216,128]{1,0:T(8,128)S(1)} %pad_maximum_fusion), channel_id=1, source_target_pairs={{0,32},{32,64},{64,96},{96,0},{1,33},{33,65},{65,97},{97,1},{2,34}... | collective-permute-start | bytes 331784 | tf_op jit(solution)/shard_map/ppermute | solution.py:342
  50.6 0.5 collective-permute-done.3
  51.0 0.0 copy-start.8
  51.1 0.0 copy-start.9
  51.1 0.1 collective-permute-start.4
  51.2 2.1 %collective-permute-done.2.r1_ref = f32[216,128]{1,0:T(8,128)S(1)} collective-permute-done((f32[216,128]{1,0:T(8,128)S(1)}, f32[216,128]{1,0:T(8,128)S(1)}, u32[]{:S(2)}, u32[]{:S(2)}) %collective-permute-start.2) | collective-permute-done | bytes 110624 | tf_op jit(solution)/shard_map/ppermute | solution.py:342
  53.3 6.3 %collective-permute-done.4.r2_ref = f32[216,128]{1,0:T(8,128)S(1)} collective-permute-done((f32[216,128]{1,0:T(8,128)S(1)}, f32[216,128]{1,0:T(8,128)S(1)}, u32[]{:S(2)}, u32[]{:S(2)}) %collective-permute-start.4) | collective-permute-done | bytes 110624 | tf_op jit(solution)/shard_map/ppermute | solution.py:343
  59.7 0.7 second.1
  60.3 0.0 copy-start.6
  60.4 0.0 copy-start.7
  60.4 12.5 %all_to_all.11.r_ref = f32[32,16,128]{2,1,0:T(8,128)S(1)} all-to-all(f32[32,16,128]{2,1,0:T(8,128)S(1)} %second.1), channel_id=1, replica_groups=mesh['yh'=2,'zh'=4,'zl'=2,'core'=2,'x'=4,'yl'=2] {'yh','x','yl','zl'}, dimensions={0} | all-to-all | bytes 524288 | tf_op jit(solution)/shard_map/all_to_all | solution.py:352
  72.9 1.4 %third.1 = f32[9,36,288]{2,1,0:T(8,128)} custom-call(f32[32,16,128]{2,1,0:T(8,128)S(1)} %all_to_all.11.r_ref, bf16[160,288]{1,0:T(8,128)(2,1)S(1)} %copy-done.7, bf16[160,288]{1,0:T(8,128)(2,1)S(1)} %copy-done.6), custom_call_target="tpu_custom_call" | custom-call | flops 1000000000 | bytes 2000000 | tf_op jit(solution)/shard_map/third/pallas_call | solution.py:353
  (22 shorter events, 0.1 us)
Async XLA Ops:
  0.0 0.7 copy-start
  2.0 1.0 %copy-start.2 = (bf16[320,432]{1,0:T(8,128)(2,1)S(1)}, bf16[320,432]{1,0:T(8,128)(2,1)}, u32[]{:S(2)}) copy-start(bf16[320,432]{1,0:T(8,128)(2,1)} %constant.68.clone.w_ref) | copy-start | bytes 829444
  3.5 25.1 %copy-start.1 = (bf16[2,160,432]{2,1,0:T(8,128)(2,1)S(1)}, bf16[2,160,432]{2,1,0:T(8,128)(2,1)}, u32[]{:S(2)}) copy-start(bf16[2,160,432]{2,1,0:T(8,128)(2,1)} %constant.72.clone.ug_ref) | copy-start | bytes 829444
  3.6 25.1 %copy-start.3 = (bf16[288,432]{1,0:T(8,128)(2,1)S(1)}, bf16[288,432]{1,0:T(8,128)(2,1)}, u32[]{:S(2)}) copy-start(bf16[288,432]{1,0:T(8,128)(2,1)} %constant.71.clone.er_ref) | copy-start | bytes 746500
  3.6 25.1 %copy-start.4 = (bf16[256,384]{1,0:T(8,128)(2,1)S(1)}, bf16[256,384]{1,0:T(8,128)(2,1)}, u32[]{:S(2)}) copy-start(bf16[256,384]{1,0:T(8,128)(2,1)} %constant.70.clone.elo_ref) | copy-start | bytes 589828
  3.6 25.1 %copy-start.5 = (bf16[256,384]{1,0:T(8,128)(2,1)S(1)}, bf16[256,384]{1,0:T(8,128)(2,1)}, u32[]{:S(2)}) copy-start(bf16[256,384]{1,0:T(8,128)(2,1)} %constant.69.clone.ehi_ref) | copy-start | bytes 589828
  38.5 1.9 %collective-permute-start = (f32[4,216,128]{2,1,0:T(8,128)S(1)}, f32[4,216,128]{2,1,0:T(8,128)S(1)}, u32[]{:S(2)}, u32[]{:S(2)}) collective-permute-start(f32[4,216,128]{2,1,0:T(8,128)S(1)} %get-tuple-element.11), channel_id=1, source_target_pairs={{0,8},{8,0},{1,9},{9,1},{2,10},{10,2},{3,11},{11,3},{4,12},{12,4},... | collective-permute-start | bytes 1327112 | tf_op jit(solution)/shard_map/ppermute | solution.py:334
  40.5 5.9 %collective-permute-start.1 = (f32[104,128]{1,0:T(8,128)S(1)}, f32[104,128]{1,0:T(8,128)S(1)}, u32[]{:S(2)}, u32[]{:S(2)}) collective-permute-start(f32[104,128]{1,0:T(8,128)S(1)} %slice.44), channel_id=1, source_target_pairs={{0,32},{32,64},{64,96},{96,0},{1,33},{33,65},{65,97},{97,1},{2,34}... | collective-permute-start | bytes 159752 | tf_op jit(solution)/shard_map/ppermute | solution.py:336
  44.2 6.8 %collective-permute-start.3 = (f32[112,128]{1,0:T(8,128)S(1)}, f32[112,128]{1,0:T(8,128)S(1)}, u32[]{:S(2)}, u32[]{:S(2)}) collective-permute-start(f32[112,128]{1,0:T(8,128)S(1)} %slice.49), channel_id=1, source_target_pairs={{0,96},{32,0},{64,32},{96,64},{1,97},{33,1},{65,33},{97,65},{2,98}... | collective-permute-start | bytes 172040 | tf_op jit(solution)/shard_map/ppermute | solution.py:337
  46.4 13.3 %copy-start.10 = (bf16[128,384]{1,0:T(8,128)(2,1)S(1)}, bf16[128,384]{1,0:T(8,128)(2,1)}, u32[]{:S(2)}) copy-start(bf16[128,384]{1,0:T(8,128)(2,1)} %constant.74.clone.flo_ref) | copy-start | bytes 294916
  46.4 13.3 %copy-start.11 = (bf16[128,384]{1,0:T(8,128)(2,1)S(1)}, bf16[128,384]{1,0:T(8,128)(2,1)}, u32[]{:S(2)}) copy-start(bf16[128,384]{1,0:T(8,128)(2,1)} %constant.73.clone.fhi_ref) | copy-start | bytes 294916
  46.4 6.9 %collective-permute-start.2 = (f32[216,128]{1,0:T(8,128)S(1)}, f32[216,128]{1,0:T(8,128)S(1)}, u32[]{:S(2)}, u32[]{:S(2)}) collective-permute-start(f32[216,128]{1,0:T(8,128)S(1)} %pad_maximum_fusion), channel_id=1, source_target_pairs={{0,32},{32,64},{64,96},{96,0},{1,33},{33,65},{65,97},{97,1},{2,34}... | collective-permute-start | bytes 331784 | tf_op jit(solution)/shard_map/ppermute | solution.py:342
  51.0 8.6 %copy-start.8 = (bf16[128,384]{1,0:T(8,128)(2,1)S(1)}, bf16[128,384]{1,0:T(8,128)(2,1)}, u32[]{:S(2)}) copy-start(bf16[128,384]{1,0:T(8,128)(2,1)} %constant.76.clone.tlo_ref) | copy-start | bytes 294916
  51.1 8.6 %copy-start.9 = (bf16[128,384]{1,0:T(8,128)(2,1)S(1)}, bf16[128,384]{1,0:T(8,128)(2,1)}, u32[]{:S(2)}) copy-start(bf16[128,384]{1,0:T(8,128)(2,1)} %constant.75.clone.thi_ref) | copy-start | bytes 294916
  51.1 8.6 %collective-permute-start.4 = (f32[216,128]{1,0:T(8,128)S(1)}, f32[216,128]{1,0:T(8,128)S(1)}, u32[]{:S(2)}, u32[]{:S(2)}) collective-permute-start(f32[216,128]{1,0:T(8,128)S(1)} %pad_maximum_fusion.1), channel_id=1, source_target_pairs={{0,96},{32,0},{64,32},{96,64},{1,97},{33,1},{65,33},{97,65},{2,98}... | collective-permute-start | bytes 331784 | tf_op jit(solution)/shard_map/ppermute | solution.py:343
  60.3 12.6 %copy-start.6 = (bf16[160,288]{1,0:T(8,128)(2,1)S(1)}, bf16[160,288]{1,0:T(8,128)(2,1)}, u32[]{:S(2)}) copy-start(bf16[160,288]{1,0:T(8,128)(2,1)} %constant.78.clone.ulo_ref) | copy-start | bytes 276484
  60.4 12.6 %copy-start.7 = (bf16[160,288]{1,0:T(8,128)(2,1)S(1)}, bf16[160,288]{1,0:T(8,128)(2,1)}, u32[]{:S(2)}) copy-start(bf16[160,288]{1,0:T(8,128)(2,1)} %constant.77.clone.uhi_ref) | copy-start | bytes 276484
